TPU v7x, 256 devices: a whole 4x4x8 slice. The times are simulated.
256 devices in a mesh: gx: 8 (over x, y_hi), gy: 4 (over y_lo, core), gz: 8 (over z).
Axes of the slice: x: 4, y: 4 (y_hi: 2, y_lo: 2; y = y_hi * 2 + y_lo), z: 8, core: 2. Of those that a mesh axis runs over, the one named last changes fastest.
Arguments:
- density: float32 [40, 20, 1280], P('gx', 'gy', 'gz'), may hold values from 0.5 to 2
- velocity: float32 [3, 40, 20, 1280], P(None, 'gx', 'gy', 'gz'), may hold values from -3.2 to 3.2
- pressure: float32 [40, 20, 1280], P('gx', 'gy', 'gz'), may hold values from 0.5 to 2
- blending: float32 [8, 4, 256], P('gx', 'gy', 'gz'), may hold values from 0 to 0.6
- face_signal_weights: bfloat16 [4, 10240, 4096], P(None, ('gx', 'gy'), 'gz'), may hold values from -0.013671875 to 0.013671875
- surf_id: int32 [30720], P(('gx', 'gy', 'gz')), may hold values from -1 to 10239, as said below
- surface_face_code: int32 [30720], P(('gx', 'gy', 'gz')), may hold values from 0 to 191, as said below
Outputs:
- tendency: float32 [5, 40, 20, 1280], P(None, 'gx', 'gy', 'gz')
- signals: float32 [4096], P(('gz', 'gx', 'gy'))
Inputs may be any that keep to these rules, and one draw needn't show every extreme that they name: `surf_id`: every face id 0 to 10239 stands in exactly one slot; a device's listed faces fill its first slots and its other slots hold -1. A quarter of the devices list exactly 120 faces, the others at most 40. `surface_face_code`: the codes of one device are distinct.
All inputs are finite; a program needn't handle non-finite values.
Results may differ from a plain program's by a relative error of at most 0.0029.
Values may be sent and summed in bfloat16 or wider, within the bound.
No kernel may reach another device: no remote copies, remote signals or barrier semaphores. Data moves between devices by JAX's collectives and lax.ppermute only.
A program may use at most 128 MiB of HBM per device.

v0:
```python
import functools
import math

import jax
import jax.numpy as jnp
import numpy as np
from jax import lax
from jax.experimental import pallas as pl
from jax.experimental.pallas import tpu as pltpu
from jax.sharding import PartitionSpec as P


GAMMA = 1.4
NODES = 5
PAIR = ("gx", "gy")
LANES = 256
F32 = jnp.float32
BF16 = jnp.bfloat16


def gauss_lobatto():
    inner_root = math.sqrt(3.0 / 7.0)
    points = np.array([-1.0, -inner_root, 0.0, inner_root, 1.0])
    quad_weights = np.array([0.1, 49.0 / 90.0, 32.0 / 45.0, 49.0 / 90.0, 0.1])
    barycentric = np.ones(5)
    for target in range(5):
        for source in range(5):
            if source != target:
                barycentric[target] = barycentric[target] / (points[target] - points[source])
    derivative = np.zeros((5, 5))
    for target in range(5):
        for source in range(5):
            if source != target:
                derivative[target, source] = (
                    barycentric[source] / barycentric[target] / (points[target] - points[source])
                )
        derivative[target, target] = -np.sum(derivative[target])
    return (derivative, quad_weights)


DERIV, WEIGHTS = gauss_lobatto()


def iota(shape, dim):
    return lax.broadcasted_iota(jnp.int32, shape, dim)


def by_node(node, values):
    picked = jnp.zeros(node.shape, F32)
    for n, value in enumerate(values):
        if value != 0.0:
            picked = jnp.where(node == n, F32(value), picked)
    return picked


def flux4(rho, vel, pressure, d):
    mass = rho * vel[d]
    return [mass] + [mass * vel[m] + pressure if m == d else mass * vel[m] for m in range(3)]


def lay_out(den, vel, pre, grid):
    nx, ny, nz = den.shape
    for x in range(nx):
        grid[0, x, 0:ny, 0:nz] = den[x]
        grid[4, x, 0:ny, 0:nz] = pre[x]
        for y in range(ny):
            for m in range(3):
                grid[1 + m, x, y : y + 1, 0:nz] = vel[x, y, m : m + 1, :]


def face_kernel(per_group, den, vel, pre, sid, code, blocks, x_lo, x_hi, y_lo, y_hi, z_both, grid, rows, den_v, vel_v, pre_v, sid_v, code_v, sems):
    pairs = ((den, den_v), (vel, vel_v), (pre, pre_v), (sid, sid_v), (code, code_v))
    loads = [pltpu.make_async_copy(src, dst, sems.at[i]) for i, (src, dst) in enumerate(pairs)]
    for load in loads:
        load.start()
    nx, ny, nz = den.shape
    slots = sid.shape[1]
    groups = blocks.shape[0]
    rows[...] = jnp.zeros_like(rows)
    for load in loads:
        load.wait()

    lay_out(den_v, vel_v, pre_v, grid)

    def field(f, x):
        return grid[f, x, 0:ny, 0:nz]

    wy = by_node(iota((ny, nz), 0), WEIGHTS)

    sum_y = [None] * 4
    sum_z = [None] * 4
    for x in range(nx):
        rho, v, p = field(0, x), [field(1 + m, x) for m in range(3)], field(4, x)
        for q, value in enumerate(flux4(rho, v, p, 1)):
            term = F32(WEIGHTS[x]) * value
            sum_y[q] = term if sum_y[q] is None else sum_y[q] + term
        for q, value in enumerate(flux4(rho, v, p, 2)):
            term = F32(WEIGHTS[x]) * value
            sum_z[q] = term if sum_z[q] is None else sum_z[q] + term
        if x in (0, nx - 1):
            side, sign = (0, -1.0) if x == 0 else (1, 1.0)
            for q, value in enumerate(flux4(rho, v, p, 0)):
                rows[8 * q + side : 8 * q + side + 1, :] = F32(sign) * jnp.sum(wy * value, axis=0, keepdims=True)
    for q in range(4):
        rows[8 * q + 2 : 8 * q + 3, :] = -sum_y[q][0:1]
        rows[8 * q + 3 : 8 * q + 4, :] = sum_y[q][ny - 1 : ny]
        over_z = jnp.sum(wy * sum_z[q], axis=0, keepdims=True)
        rows[8 * q + 4 : 8 * q + 5, :] = -over_z
        rows[8 * q + 5 : 8 * q + 6, :] = over_z

    face = lax.shift_right_logical(code_v[...], 5)
    elem = code_v[...] & 31
    z = iota((nz, slots), 0)
    z_elem = lax.shift_right_logical(z * 52429, 18)
    z_node = z - 5 * z_elem
    plane = jnp.where(z_node == 4 * (face - 4), F32(1), F32(0))
    pick = jnp.where(z_elem == elem, jnp.where(face < 4, by_node(z_node, WEIGHTS), plane), F32(0))
    by_face = jnp.dot(rows[...], pick, precision=lax.Precision.HIGHEST, preferred_element_type=F32)
    face_hot = iota((8, slots), 0) == face
    data = [
        jnp.sum(jnp.where(face_hot, by_face[8 * q : 8 * q + 8], F32(0)), axis=0, keepdims=True)
        for q in range(4)
    ]

    ids = sid_v[...]
    group = lax.shift_right_logical(jnp.maximum(ids, 0) * 6554, 21)
    offset = ids - per_group * group
    chunk = lax.shift_right_logical(jnp.maximum(offset, 0), 7)
    group = jnp.where(ids >= 0, group, -1)
    row = iota((16, slots), 0)
    row_q = lax.shift_right_logical(row * 21846, 16)
    spread = jnp.zeros((16, slots), F32)
    for q in range(4):
        spread = jnp.where(row_q == q, data[q], spread)
    spread = jnp.where(row - 3 * row_q == chunk, spread, F32(0)).astype(BF16).astype(F32)
    group_of = iota((groups, 16, slots), 0)
    spread = jnp.where(group_of == group[None], spread[None], F32(0))
    spread = spread.reshape(groups * 16, slots).astype(BF16)
    lane_hot = (iota((128, slots), 0) == (offset & 127)).astype(F32).astype(BF16)
    placed = lax.dot_general(spread, lane_hot, (((1,), (1,)), ((), ())), preferred_element_type=F32)
    blocks[...] = placed.astype(BF16).reshape(groups, 16, 128)

    for f in range(5):
        x_lo[f] = grid[f, 0, 0:ny, 0:nz]
        x_hi[f] = grid[f, nx - 1, 0:ny, 0:nz]
        for x in range(nx):
            y_lo[f, x : x + 1] = grid[f, x, 0:1, 0:nz]
            y_hi[f, x : x + 1] = grid[f, x, ny - 1 : ny, 0:nz]

    z_both[...] = jnp.zeros_like(z_both)
    packed = jnp.zeros((ny, 128), F32)
    lane = iota((ny, 128), 1)
    for f in range(5):
        for x in range(nx):
            at = 5 * f + x
            packed = jnp.where(lane == at, grid[f, x, 0:ny, 0:1], packed)
            packed = jnp.where(lane == 64 + at, grid[f, x, 0:ny, nz - 1 : nz], packed)
    z_both[0:ny] = packed


def split_flux(a, b, d):
    half = [F32(0.5) * (x + y) for x, y in zip(a, b)]
    rho, vel, pressure, specific = half[0], half[1:4], half[4], half[5]
    mass = rho * vel[d]
    out = [mass]
    for m in range(3):
        value = mass * vel[m]
        out.append(value + pressure if m == d else value)
    out.append(mass * specific + pressure * vel[d])
    return out


def node_parts(a, d):
    rho, vel, pressure, specific, sound = a[0], a[1:4], a[4], a[5], a[6]
    cons = [rho] + [rho * v for v in vel] + [rho * specific]
    mass = cons[1 + d]
    flux = [mass] + [mass * vel[m] + pressure if m == d else mass * vel[m] for m in range(3)]
    flux.append((cons[4] + pressure) * vel[d])
    return flux, cons, jnp.abs(vel[d]) + sound


def rusanov(left, right):
    speed = F32(0.5) * jnp.maximum(left[2], right[2])
    return [
        F32(0.5) * (fl + fr) - speed * (ur - ul)
        for fl, fr, ul, ur in zip(left[0], right[0], left[1], right[1])
    ]


def derived(rho, v1, v2, v3, pressure):
    inverse = F32(1) / rho
    ratio = pressure * inverse
    specific = ratio * F32(1.0 / (GAMMA - 1.0)) + F32(0.5) * (v1 * v1 + v2 * v2 + v3 * v3)
    return [rho, v1, v2, v3, pressure, specific, jnp.sqrt(F32(GAMMA) * ratio)]


def tendency_kernel(start, blend, x_low, x_up, y_low, y_up, z_all, out, grid):
    _, nx, ny, nz = out.shape
    shape = (8, LANES)
    grid[...] = jnp.ones_like(grid)
    layers = z_all.shape[0]
    here = lax.axis_index("gz")
    z_low = z_all[lax.rem(here + layers - 1, layers), 16:24]
    z_up = z_all[lax.rem(here + 1, layers), 16:24]
    half_lane = iota((8, 128), 1)
    outside = (iota((8, 128), 0) >= ny) & (half_lane >= nz - 128)
    for f in range(5):
        grid[f, 0, 0:ny, 0:nz] = x_low[f]
        grid[f, 1 + nx, 0:ny, 0:nz] = x_up[f]
        for x in range(nx):
            grid[f, 1 + x, 0:ny, 0:nz] = start[f, x, 0:ny, 0:nz]
            grid[f, 1 + x, ny : ny + 1, 0:nz] = y_up[f, x : x + 1]
            grid[f, 1 + x, 7:8, 0:nz] = y_low[f, x : x + 1]
            at = 5 * f + x
            upper = grid[f, 1 + x, :, 128:256]
            upper = jnp.where(half_lane == nz - 128, pltpu.roll(z_up, (nz - 128 - at) % 128, 1), upper)
            upper = jnp.where(half_lane == 127, pltpu.roll(z_low, (127 - 64 - at) % 128, 1), upper)
            upper = jnp.where(outside, F32(1), upper)
            grid[f, 1 + x, :, 128:256] = upper

    def state(x):
        return derived(*[grid[f, 1 + x] for f in range(5)])

    row = iota(shape, 0)
    lane = iota(shape, 1)
    lane_elem = lax.shift_right_logical(lane * 52429, 18)
    node = lane - 5 * lane_elem
    elems = blend.shape[1]
    spread = (iota((elems, LANES), 0) == lax.shift_right_logical(iota((elems, LANES), 1) * 52429, 18)).astype(F32)
    alpha = jnp.dot(
        jnp.broadcast_to(blend[...], (8, elems)), spread, precision=lax.Precision.HIGHEST, preferred_element_type=F32
    )
    keep = F32(1) - alpha
    inv = 1.0 / WEIGHTS

    def sides(index):
        inverse = by_node(index, inv)
        up = inverse * jnp.where(index == NODES - 1, F32(1), alpha)
        low = inverse * jnp.where(index == 0, F32(1), alpha)
        return up, low

    def pair_factors(index):
        ups = [by_node(index, [2.0 * DERIV[i, i + k] if i + k < NODES else 0.0 for i in range(NODES)]) for k in range(1, NODES)]
        downs = [by_node(index, [2.0 * DERIV[i, i - k] if i >= k else 0.0 for i in range(NODES)]) for k in range(1, NODES)]
        return ups, downs

    states = [state(x) for x in range(-1, nx + 1)]
    parts = [node_parts(s, 0) for s in states]
    faces = [rusanov(parts[i], parts[i + 1]) for i in range(nx + 1)]
    high = [[None] * 5 for _ in range(nx)]
    for i in range(nx):
        for j in range(i + 1, nx):
            pair = split_flux(states[1 + i], states[1 + j], 0)
            for c in range(5):
                for target, source in ((i, j), (j, i)):
                    term = F32(2.0 * DERIV[target, source]) * pair[c]
                    high[target][c] = term if high[target][c] is None else high[target][c] + term
    total = [[None] * 5 for _ in range(nx)]
    for x in range(nx):
        up = F32(inv[x]) if x == nx - 1 else F32(inv[x]) * alpha
        low = F32(inv[x]) if x == 0 else F32(inv[x]) * alpha
        for c in range(5):
            total[x][c] = keep * high[x][c] + (up * faces[x + 1][c] - low * faces[x][c])

    for d, axis, size, index in ((1, 0, 8, row), (2, 1, LANES, node)):
        ups, downs = pair_factors(index)
        up, low = sides(index)
        for x in range(nx):
            node_here = states[1 + x]
            high_x = [None] * 5
            for k in range(1, NODES):
                there = [pltpu.roll(s, size - k, axis) for s in (node_here if k == 1 else node_here[:6])]
                pair = split_flux(node_here[:6], there[:6], d)
                for c in range(5):
                    term = ups[k - 1] * pair[c] + downs[k - 1] * pltpu.roll(pair[c], k, axis)
                    high_x[c] = term if high_x[c] is None else high_x[c] + term
                if k == 1:
                    face = rusanov(node_parts(node_here, d), node_parts(there, d))
                    edge = [up * f - low * pltpu.roll(f, 1, axis) for f in face]
            for c in range(5):
                total[x][c] = total[x][c] + (keep * high_x[c] + edge[c])
    for x in range(nx):
        for c in range(5):
            out[c, x] = (-total[x][c])[0:ny, 0:nz]


def gather_kernel(got, z_both, copies):
    total = got[0].astype(F32)
    for i in range(1, got.shape[0]):
        total = total + got[i].astype(F32)
    for i in range(copies.shape[0]):
        copies[i, 0:16] = total
        copies[i, 16:24] = z_both[...]


def keep_kernel(array, kept):
    kept[...] = array[...]


def signal_kernel(got, weights, out):
    blocks = jnp.zeros((got.shape[0], weights.shape[2]), F32)
    faces = weights.shape[1]
    for q in range(weights.shape[0]):
        for c in range(3):
            width = min(128, faces - 128 * c)
            data = got[:, 3 * q + c, 0:width].astype(BF16)
            blocks = blocks + jnp.dot(data, weights[q, 128 * c : 128 * c + width, :], preferred_element_type=F32)
    total = jnp.sum(blocks, axis=0, keepdims=True)
    size = out.shape[2]
    for g in range(out.shape[0]):
        out[g] = total[:, g * size : (g + 1) * size]


def sum_kernel(tiles, out):
    total = tiles[0]
    for g in range(1, tiles.shape[0]):
        total = total + tiles[g]
    out[...] = total


def call(kernel, outs, args, scratch=(), flops=1_000_000, hbm=(), limit=16, aliases=None):
    single = not isinstance(outs, (list, tuple))
    inside = pl.BlockSpec(memory_space=pltpu.VMEM)
    return pl.pallas_call(
        kernel,
        out_shape=outs,
        in_specs=[pl.BlockSpec(memory_space=pltpu.HBM) if i in hbm else inside for i in range(len(args))],
        out_specs=inside if single else [inside] * len(outs),
        scratch_shapes=scratch,
        input_output_aliases=aliases or {},
        compiler_params=pltpu.CompilerParams(vmem_limit_bytes=limit * 1024 * 1024),
        cost_estimate=pl.CostEstimate(flops=flops, bytes_accessed=200_000, transcendentals=0),
    )(*args)


def step(density, velocity, pressure, blending, face_signal_weights, surf_id, surface_face_code):
    nx, ny, nz = density.shape
    sds = jax.ShapeDtypeStruct
    groups = lax.axis_size("gx") * lax.axis_size("gy")
    layers = lax.axis_size("gz")
    _, faces, local = face_signal_weights.shape
    ids = surf_id.reshape(1, -1)
    codes = surface_face_code.reshape(1, -1)
    slots = ids.shape[1]
    speeds = jnp.transpose(velocity, (1, 2, 0, 3))
    blocks, x_lo, x_hi, y_lo, y_hi, z_both, grid = call(
        functools.partial(face_kernel, faces),
        [sds((groups, 16, 128), BF16)]
        + [sds((5, ny, nz), F32)] * 2
        + [sds((5, nx, nz), F32)] * 2
        + [sds((8, 128), F32), sds((5, nx, 8, LANES), F32)],
        [density, speeds, pressure, ids, codes],
        [
            pltpu.VMEM((32, nz), F32),
            pltpu.VMEM((nx, ny, nz), F32),
            pltpu.VMEM((nx, ny, 3, nz), F32),
            pltpu.VMEM((nx, ny, nz), F32),
            pltpu.VMEM((1, slots), jnp.int32),
            pltpu.VMEM((1, slots), jnp.int32),
            pltpu.SemaphoreType.DMA((5,)),
        ],
        hbm=(0, 1, 2, 3, 4),
        limit=60,
    )
    arrived = lax.all_to_all(blocks, PAIR, 0, 0, tiled=True)
    held = call(
        keep_kernel, sds(face_signal_weights.shape, BF16), [face_signal_weights], flops=2_000_000
    )
    z_kept = call(keep_kernel, sds(z_both.shape, F32), [z_both])

    def shift(array, axis, step):
        peers = lax.axis_size(axis)
        return lax.ppermute(array, axis, [(i, (i + step) % peers) for i in range(peers)])

    x_low = shift(x_hi, "gx", 1)
    x_up = shift(x_lo, "gx", -1)
    y_low = shift(y_hi, "gy", 1)
    y_up = shift(y_lo, "gy", -1)

    copies = call(gather_kernel, sds((layers, 24, 128), F32), [arrived, z_kept])
    everywhere = lax.all_to_all(copies, "gz", 0, 0, tiled=True)
    partial = call(signal_kernel, sds((groups, 1, local // groups), F32), [everywhere, held])
    tiles = lax.all_to_all(partial, PAIR, 0, 0, tiled=True)
    signals = call(sum_kernel, sds((1, local // groups), F32), [tiles]).reshape(-1)

    tendency = call(
        tendency_kernel,
        sds((5, nx, ny, nz), F32),
        [grid, blending.reshape(1, -1), x_low, x_up, y_low, y_up, everywhere],
        [pltpu.VMEM((5, nx + 2, 8, LANES), F32)],
        flops=20_000_000,
    )
    return (tendency, signals)


def solution(mesh):
    placed = (
        P("gx", "gy", "gz"),
        P(None, "gx", "gy", "gz"),
        P("gx", "gy", "gz"),
        P("gx", "gy", "gz"),
        P(None, ("gx", "gy"), "gz"),
        P(("gx", "gy", "gz")),
        P(("gx", "gy", "gz")),
    )
    return jax.shard_map(
        step,
        mesh=mesh,
        in_specs=placed,
        out_specs=(P(None, "gx", "gy", "gz"), P(("gz", "gx", "gy"))),
        check_vma=False,
    )
```

profile of v0, /device:TPU:1, one launch (start us, length us, event | category | flops | bytes accessed | tf_op | source)
XLA Modules:
  0.0 49.6 jit_solution(14232558043375349365)
XLA Ops:
  0.6 2.2 %shard_map.86 = (bf16[32,16,128]{2,1,0:T(8,128)(2,1)}, f32[5,5,160]{2,1,0:T(8,128)}, f32[5,5,160]{2,1,0:T(8,128)}, f32[5,5,160]{2,1,0:T(8,128)}, f32[5,5,160]{2,...) custom-call(f32[5,5,160]{2,1,0:T(8,128)} %den.1, f32[5,5,3,160]{3,2,1,0:T(4,128)} %bitcast.6, f32[5,5,160]{2,1,0:T(8,128)} %pre.1, ...), custom_call_target="tpu_custom_call" | custom-call | flops 1000000 | bytes 200000 | tf_op jit(solution)/shard_map/pallas_call | solution.py:324
  2.9 8.6 %all-to-all-start = ((bf16[32,16,128]{2,1,0:T(8,128)(2,1)}), bf16[32,16,128]{2,1,0:T(8,128)(2,1)S(1)}, u32[]{:S(2)}, u32[]{:S(2)}) async-start(bf16[32,16,128]{2,1,0:T(8,128)(2,1)} %get-tuple-element.14), calls=%async_computation | async-start | bytes 262144 | tf_op jit(solution)/shard_map/all_to_all | solution.py:365
  11.5 0.0 copy-start.2
  11.5 0.7 %copy-done.2 = f32[8,128]{1,0:T(8,128)S(1)} copy-done((f32[8,128]{1,0:T(8,128)S(1)}, f32[8,128]{1,0:T(8,128)}, u32[]{:S(2)}) %copy-start.2) | copy-done | bytes 4120
  12.1 7.0 %all-to-all-done.got = bf16[32,16,128]{2,1,0:T(8,128)(2,1)S(1)} async-done(((bf16[32,16,128]{2,1,0:T(8,128)(2,1)}), bf16[32,16,128]{2,1,0:T(8,128)(2,1)S(1)}, u32[]{:S(2)}, u32[]{:S(2)}) %all-to-all-start) | async-done | bytes 131104 | tf_op jit(solution)/shard_map/all_to_all | solution.py:365
  19.1 0.7 %shard_map.88 = f32[8,24,128]{2,1,0:T(8,128)} custom-call(bf16[32,16,128]{2,1,0:T(8,128)(2,1)S(1)} %all-to-all-done.got, f32[8,128]{1,0:T(8,128)S(1)} %shard_map.87.z_both), custom_call_target="tpu_custom_call" | custom-call | flops 1000000 | bytes 200000 | tf_op jit(solution)/shard_map/pallas_call | solution.py:324
  19.8 8.2 %all-to-all-start.1 = ((f32[8,24,128]{2,1,0:T(8,128)}), f32[8,24,128]{2,1,0:T(8,128)S(1)}, u32[]{:S(2)}, u32[]{:S(2)}) async-start(f32[8,24,128]{2,1,0:T(8,128)} %shard_map.88), calls=%async_computation.1 | async-start | bytes 196608 | tf_op jit(solution)/shard_map/all_to_all | solution.py:381
  28.0 0.7 %collective-permute-start = (f32[5,5,160]{2,1,0:T(8,128)}, f32[5,5,160]{2,1,0:T(8,128)S(1)}, u32[]{:S(2)}, u32[]{:S(2)}) collective-permute-start(f32[5,5,160]{2,1,0:T(8,128)} %get-tuple-element.10), channel_id=1, source_target_pairs={{0,32},{32,64},{64,96},{96,128},{128,160},{160,192},{192,224},{224... | collective-permute-start | bytes 48008 | tf_op jit(solution)/shard_map/ppermute | solution.py:373
  28.7 4.4 %collective-permute-start.1 = (f32[5,5,160]{2,1,0:T(8,128)}, f32[5,5,160]{2,1,0:T(8,128)S(1)}, u32[]{:S(2)}, u32[]{:S(2)}) collective-permute-start(f32[5,5,160]{2,1,0:T(8,128)} %get-tuple-element.11), channel_id=1, source_target_pairs={{0,224},{32,0},{64,32},{96,64},{128,96},{160,128},{192,160},{224,1... | collective-permute-start | bytes 48008 | tf_op jit(solution)/shard_map/ppermute | solution.py:373
  33.1 1.4 %collective-permute-start.2 = (f32[5,5,160]{2,1,0:T(8,128)}, f32[5,5,160]{2,1,0:T(8,128)S(1)}, u32[]{:S(2)}, u32[]{:S(2)}) collective-permute-start(f32[5,5,160]{2,1,0:T(8,128)} %get-tuple-element.12), channel_id=1, source_target_pairs={{0,8},{8,16},{16,24},{24,0},{1,9},{9,17},{17,25},{25,1},{2,10},{10... | collective-permute-start | bytes 48008 | tf_op jit(solution)/shard_map/ppermute | solution.py:373
  34.4 0.0 collective-permute-start.3
  34.4 0.0 copy-start
  34.4 1.3 %copy-done = bf16[4,320,512]{2,1,0:T(8,128)(2,1)S(1)} copy-done((bf16[4,320,512]{2,1,0:T(8,128)(2,1)S(1)}, bf16[4,320,512]{2,1,0:T(8,128)(2,1)}, u32[]{:S(2)}) %copy-start) | copy-done | bytes 1310744
  35.8 0.1 shard_map.90.weights
  35.9 0.0 copy-start.1
  35.9 0.0 copy-start.3
  35.9 0.0 all-to-all-done.1.z_all.got
  35.9 1.0 %shard_map.91 = f32[32,1,16]{2,1,0:T(1,128)} custom-call(f32[8,24,128]{2,1,0:T(8,128)S(1)} %all-to-all-done.1.z_all.got, bf16[4,320,512]{2,1,0:T(8,128)(2,1)S(1)} %shard_map.90.weights), custom_call_target="tpu_custom_call" | custom-call | flops 1000000 | bytes 200000 | tf_op jit(solution)/shard_map/pallas_call | solution.py:324
  36.9 5.1 %all-to-all-start.2 = ((f32[32,1,16]{2,1,0:T(1,128)}), f32[32,1,16]{2,1,0:T(1,128)S(1)}, u32[]{:S(2)}, u32[]{:S(2)}) async-start(f32[32,1,16]{2,1,0:T(1,128)} %shard_map.91), calls=%async_computation.2 | async-start | bytes 32768 | tf_op jit(solution)/shard_map/all_to_all | solution.py:383
  42.0 0.0 collective-permute-done.x_low
  42.0 0.0 collective-permute-done.1.x_up
  42.0 0.0 collective-permute-done.2.y_low
  42.0 0.0 collective-permute-done.3.y_up
  42.0 0.0 copy-done.1
  42.0 0.0 copy-done.3
  42.0 2.3 %shard_map.89 = f32[5,5,5,160]{3,2,1,0:T(8,128)} custom-call(f32[5,5,8,256]{3,2,1,0:T(8,128)S(1)} %copy-done.1, f32[1,32]{1,0:T(1,128)S(1)} %bitcast.5, f32[5,5,160]{2,1,0:T(8,128)S(1)} %collective-permute-done.x_low, f32[5,5,160]{2,1,0:T(8,128)S(1)} %collective-permute-done.1.x_up, f32[5,5,160]{2,1,0:T(8,128)S(1)} %collective-permute-done.2.y_low, ...), custom_call_target="tpu_custom_call" | custom-call | flops 20000000 | bytes 200000 | tf_op jit(solution)/shard_map/pallas_call | solution.py:324
  44.4 4.7 %all-to-all-done.2.tiles = f32[32,1,16]{2,1,0:T(1,128)S(1)} async-done(((f32[32,1,16]{2,1,0:T(1,128)}), f32[32,1,16]{2,1,0:T(1,128)S(1)}, u32[]{:S(2)}, u32[]{:S(2)}) %all-to-all-start.2) | async-done | bytes 2080 | tf_op jit(solution)/shard_map/all_to_all | solution.py:383
  49.0 0.5 %shard_map.92 = f32[1,16]{1,0:T(1,128)} custom-call(f32[32,1,16]{2,1,0:T(1,128)S(1)} %all-to-all-done.2.tiles), custom_call_target="tpu_custom_call" | custom-call | flops 1000000 | bytes 200000 | tf_op jit(solution)/shard_map/pallas_call | solution.py:324
  (1 shorter events, 0.0 us)
Async XLA Ops:
  2.9 16.3 %all-to-all-start = ((bf16[32,16,128]{2,1,0:T(8,128)(2,1)}), bf16[32,16,128]{2,1,0:T(8,128)(2,1)S(1)}, u32[]{:S(2)}, u32[]{:S(2)}) async-start(bf16[32,16,128]{2,1,0:T(8,128)(2,1)} %get-tuple-element.14), calls=%async_computation | async-start | bytes 262144 | tf_op jit(solution)/shard_map/all_to_all | solution.py:365
  11.5 0.7 %copy-start.2 = (f32[8,128]{1,0:T(8,128)S(1)}, f32[8,128]{1,0:T(8,128)}, u32[]{:S(2)}) copy-start(f32[8,128]{1,0:T(8,128)} %get-tuple-element.15.array) | copy-start | bytes 12292
  19.8 16.1 %all-to-all-start.1 = ((f32[8,24,128]{2,1,0:T(8,128)}), f32[8,24,128]{2,1,0:T(8,128)S(1)}, u32[]{:S(2)}, u32[]{:S(2)}) async-start(f32[8,24,128]{2,1,0:T(8,128)} %shard_map.88), calls=%async_computation.1 | async-start | bytes 196608 | tf_op jit(solution)/shard_map/all_to_all | solution.py:381
  28.0 14.0 %collective-permute-start = (f32[5,5,160]{2,1,0:T(8,128)}, f32[5,5,160]{2,1,0:T(8,128)S(1)}, u32[]{:S(2)}, u32[]{:S(2)}) collective-permute-start(f32[5,5,160]{2,1,0:T(8,128)} %get-tuple-element.10), channel_id=1, source_target_pairs={{0,32},{32,64},{64,96},{96,128},{128,160},{160,192},{192,224},{224... | collective-permute-start | bytes 48008 | tf_op jit(solution)/shard_map/ppermute | solution.py:373
  28.7 13.3 %collective-permute-start.1 = (f32[5,5,160]{2,1,0:T(8,128)}, f32[5,5,160]{2,1,0:T(8,128)S(1)}, u32[]{:S(2)}, u32[]{:S(2)}) collective-permute-start(f32[5,5,160]{2,1,0:T(8,128)} %get-tuple-element.11), channel_id=1, source_target_pairs={{0,224},{32,0},{64,32},{96,64},{128,96},{160,128},{192,160},{224,1... | collective-permute-start | bytes 48008 | tf_op jit(solution)/shard_map/ppermute | solution.py:373
  33.1 8.9 %collective-permute-start.2 = (f32[5,5,160]{2,1,0:T(8,128)}, f32[5,5,160]{2,1,0:T(8,128)S(1)}, u32[]{:S(2)}, u32[]{:S(2)}) collective-permute-start(f32[5,5,160]{2,1,0:T(8,128)} %get-tuple-element.12), channel_id=1, source_target_pairs={{0,8},{8,16},{16,24},{24,0},{1,9},{9,17},{17,25},{25,1},{2,10},{10... | collective-permute-start | bytes 48008 | tf_op jit(solution)/shard_map/ppermute | solution.py:373
  34.4 7.5 %collective-permute-start.3 = (f32[5,5,160]{2,1,0:T(8,128)}, f32[5,5,160]{2,1,0:T(8,128)S(1)}, u32[]{:S(2)}, u32[]{:S(2)}) collective-permute-start(f32[5,5,160]{2,1,0:T(8,128)} %get-tuple-element.13), channel_id=1, source_target_pairs={{0,24},{8,0},{16,8},{24,16},{1,25},{9,1},{17,9},{25,17},{2,26},{10... | collective-permute-start | bytes 48008 | tf_op jit(solution)/shard_map/ppermute | solution.py:373
  34.4 1.3 %copy-start = (bf16[4,320,512]{2,1,0:T(8,128)(2,1)S(1)}, bf16[4,320,512]{2,1,0:T(8,128)(2,1)}, u32[]{:S(2)}) copy-start(bf16[4,320,512]{2,1,0:T(8,128)(2,1)} %array.1) | copy-start | bytes 3932164
  35.9 6.1 %copy-start.1 = (f32[5,5,8,256]{3,2,1,0:T(8,128)S(1)}, f32[5,5,8,256]{3,2,1,0:T(8,128)}, u32[]{:S(2)}) copy-start(f32[5,5,8,256]{3,2,1,0:T(8,128)} %get-tuple-element.9.start) | copy-start | bytes 614404
  35.9 6.1 %copy-start.3 = (f32[1,1,32]{2,1,0:T(1,128)S(1)}, f32[1,1,32]{2,1,0:T(1,128)}, u32[]{:S(2)}) copy-start(f32[1,1,32]{2,1,0:T(1,128)} %param.10) | copy-start | bytes 388
  36.9 12.2 %all-to-all-start.2 = ((f32[32,1,16]{2,1,0:T(1,128)}), f32[32,1,16]{2,1,0:T(1,128)S(1)}, u32[]{:S(2)}, u32[]{:S(2)}) async-start(f32[32,1,16]{2,1,0:T(1,128)} %shard_map.91), calls=%async_computation.2 | async-start | bytes 32768 | tf_op jit(solution)/shard_map/all_to_all | solution.py:383
where the time goes:
time: 50 us; the launch traced here: 49.6 us
  starting transfers between devices  28.3 us (57%)
  waiting for transfers between devices  11.7 us (23%)
  Pallas kernels  6.86 us (14%)
  local copies, waits for them, and re-layouts  2 us (4%)
  between operations  0.74 us (1%)
    all_to_all x1, starting transfers between devices, step(): arrived = lax.all_to_all(blocks, PAIR, 0, 0, tiled=True)  8.59 us
    all_to_all x1, starting transfers between devices, step(): everywhere = lax.all_to_all(copies, 'gz', 0, 0, tiled=True)  8.19 us
    all_to_all x1, waiting for transfers between devices, step(): arrived = lax.all_to_all(blocks, PAIR, 0, 0, tiled=True)  7 us
    pallas_call x7, Pallas kernels, call(): pl.pallas_call(kernel, out_shape=outs, in_specs=[pl.BlockSpec(memory_spac...  6.86 us
    ppermute x4, starting transfers between devices, shift(): lax.ppermute(array, axis, [(i, (i + step) % peers) for i in range(peers)])  6.46 us
    all_to_all x1, starting transfers between devices, step(): tiles = lax.all_to_all(partial, PAIR, 0, 0, tiled=True)  5.06 us
    all_to_all x1, waiting for transfers between devices, step(): tiles = lax.all_to_all(partial, PAIR, 0, 0, tiled=True)  4.68 us
    unnamed x8, local copies, waits for them, and re-layouts  2 us
  transfers between devices with their start and end apart: 7, of which 2 were waited for; matrix products, arithmetic and copies ran while one was open for 0% of the time, Pallas kernels for 7%

commit v1 on v0

--- a/solution.py
+++ b/solution.py
@@ -13,6 +13,15 @@
 GAMMA = 1.4
 NODES = 5
 PAIR = ("gx", "gy")
+PLACE_FIRST = 21
+SHARE_FIRST = 4
+COLLECT_FIRST = 17
+
+
+def rotated(count, first):
+    return [(i + first) % count for i in range(count)]
+
+
 LANES = 256
 F32 = jnp.float32
 BF16 = jnp.bfloat16
@@ -126,7 +135,7 @@
     group = lax.shift_right_logical(jnp.maximum(ids, 0) * 6554, 21)
     offset = ids - per_group * group
     chunk = lax.shift_right_logical(jnp.maximum(offset, 0), 7)
-    group = jnp.where(ids >= 0, group, -1)
+    group = jnp.where(ids >= 0, (group + groups - PLACE_FIRST) & (groups - 1), -1)
     row = iota((16, slots), 0)
     row_q = lax.shift_right_logical(row * 21846, 16)
     spread = jnp.zeros((16, slots), F32)
@@ -200,8 +209,9 @@
     grid[...] = jnp.ones_like(grid)
     layers = z_all.shape[0]
     here = lax.axis_index("gz")
-    z_low = z_all[lax.rem(here + layers - 1, layers), 16:24]
-    z_up = z_all[lax.rem(here + 1, layers), 16:24]
+    at = here + 2 * layers - SHARE_FIRST
+    z_low = z_all[lax.rem(at - 1, layers), 16:24]
+    z_up = z_all[lax.rem(at + 1, layers), 16:24]
     half_lane = iota((8, 128), 1)
     outside = (iota((8, 128), 0) >= ny) & (half_lane >= nz - 128)
     for f in range(5):
@@ -308,7 +318,8 @@
     total = jnp.sum(blocks, axis=0, keepdims=True)
     size = out.shape[2]
     for g in range(out.shape[0]):
-        out[g] = total[:, g * size : (g + 1) * size]
+        at = (g + COLLECT_FIRST) % out.shape[0]
+        out[g] = total[:, at * size : (at + 1) * size]
 
 
 def sum_kernel(tiles, out):
@@ -362,7 +373,7 @@
         hbm=(0, 1, 2, 3, 4),
         limit=60,
     )
-    arrived = lax.all_to_all(blocks, PAIR, 0, 0, tiled=True)
+    arrived = lax.all_to_all(blocks, PAIR, 0, 0, tiled=True, axis_index_groups=[rotated(groups, PLACE_FIRST)])
     held = call(
         keep_kernel, sds(face_signal_weights.shape, BF16), [face_signal_weights], flops=2_000_000
     )
@@ -378,9 +389,9 @@
     y_up = shift(y_lo, "gy", -1)
 
     copies = call(gather_kernel, sds((layers, 24, 128), F32), [arrived, z_kept])
-    everywhere = lax.all_to_all(copies, "gz", 0, 0, tiled=True)
+    everywhere = lax.all_to_all(copies, "gz", 0, 0, tiled=True, axis_index_groups=[rotated(layers, SHARE_FIRST)])
     partial = call(signal_kernel, sds((groups, 1, local // groups), F32), [everywhere, held])
-    tiles = lax.all_to_all(partial, PAIR, 0, 0, tiled=True)
+    tiles = lax.all_to_all(partial, PAIR, 0, 0, tiled=True, axis_index_groups=[rotated(groups, COLLECT_FIRST)])
     signals = call(sum_kernel, sds((1, local // groups), F32), [tiles]).reshape(-1)
 
     tendency = call(

time: 50 us -> 47.5 us (0.950)
  waiting for transfers between devices: 11.7 us -> 4.11 us
  starting transfers between devices: 28.3 us -> 33.4 us
    all_to_all x3, waiting for transfers between devices: 11.7 us -> 4.1 us  [the longest x1 2.12 us: step(): lax.all_to_all(blocks, PAIR, 0, 0, tiled=True, axis_index_groups=[rotated...]
    all_to_all x3, starting transfers between devices: 21.8 us -> 25.9 us  [the longest x1 10.1 us: step(): lax.all_to_all(copies, 'gz', 0, 0, tiled=True, axis_index_groups=[rotated...]
    ppermute x4, starting transfers between devices: 6.46 us -> 7.51 us  [shift(): lax.ppermute(array, axis, [(i, (i + step) % peers) for i in range(peers)])]
where the time goes in v1:
time: 47.5 us; the launch traced here: 47.1 us
  starting transfers between devices  33.4 us (70%)
  Pallas kernels  6.86 us (14%)
  waiting for transfers between devices  4.11 us (9%)
  local copies, waits for them, and re-layouts  2 us (4%)
  between operations  0.74 us (2%)
    all_to_all x1, starting transfers between devices, step(): lax.all_to_all(copies, 'gz', 0, 0, tiled=True, axis_index_groups=[rotated...  10.1 us
    all_to_all x1, starting transfers between devices, step(): lax.all_to_all(blocks, PAIR, 0, 0, tiled=True, axis_index_groups=[rotated...  9.9 us
    ppermute x4, starting transfers between devices, shift(): lax.ppermute(array, axis, [(i, (i + step) % peers) for i in range(peers)])  7.51 us
    pallas_call x7, Pallas kernels, call(): pl.pallas_call(kernel, out_shape=outs, in_specs=[pl.BlockSpec(memory_spac...  6.86 us
    all_to_all x1, starting transfers between devices, step(): lax.all_to_all(partial, PAIR, 0, 0, tiled=True, axis_index_groups=[rotate...  5.87 us
    all_to_all x1, waiting for transfers between devices, step(): lax.all_to_all(blocks, PAIR, 0, 0, tiled=True, axis_index_groups=[rotated...  2.12 us
    unnamed x8, local copies, waits for them, and re-layouts  2 us
    all_to_all x1, waiting for transfers between devices, step(): lax.all_to_all(partial, PAIR, 0, 0, tiled=True, axis_index_groups=[rotate...  1.98 us
  transfers between devices with their start and end apart: 7, of which 2 were waited for; matrix products, arithmetic and copies ran while one was open for 0% of the time, Pallas kernels for 7%

profile of v1, /device:TPU:1, one launch (start us, length us, event | category | flops | bytes accessed | tf_op | source)
XLA Modules:
  0.0 47.1 jit_solution(3640541217929983247)
XLA Ops:
  0.6 2.2 %shard_map.86 = (bf16[32,16,128]{2,1,0:T(8,128)(2,1)}, f32[5,5,160]{2,1,0:T(8,128)}, f32[5,5,160]{2,1,0:T(8,128)}, f32[5,5,160]{2,1,0:T(8,128)}, f32[5,5,160]{2,...) custom-call(f32[5,5,160]{2,1,0:T(8,128)} %den.1, f32[5,5,3,160]{3,2,1,0:T(4,128)} %bitcast.6, f32[5,5,160]{2,1,0:T(8,128)} %pre.1, ...), custom_call_target="tpu_custom_call" | custom-call | flops 1000000 | bytes 200000 | tf_op jit(solution)/shard_map/pallas_call | solution.py:335
  2.9 9.9 %all-to-all-start = ((bf16[32,16,128]{2,1,0:T(8,128)(2,1)}), bf16[32,16,128]{2,1,0:T(8,128)(2,1)S(1)}, u32[]{:S(2)}, u32[]{:S(2)}) async-start(bf16[32,16,128]{2,1,0:T(8,128)(2,1)} %get-tuple-element.14), calls=%async_computation | async-start | bytes 262144 | tf_op jit(solution)/shard_map/all_to_all | solution.py:376
  12.8 0.0 copy-start.2
  12.8 0.7 %copy-done.2 = f32[8,128]{1,0:T(8,128)S(1)} copy-done((f32[8,128]{1,0:T(8,128)S(1)}, f32[8,128]{1,0:T(8,128)}, u32[]{:S(2)}) %copy-start.2) | copy-done | bytes 4120
  13.4 2.1 %all-to-all-done.got = bf16[32,16,128]{2,1,0:T(8,128)(2,1)S(1)} async-done(((bf16[32,16,128]{2,1,0:T(8,128)(2,1)}), bf16[32,16,128]{2,1,0:T(8,128)(2,1)S(1)}, u32[]{:S(2)}, u32[]{:S(2)}) %all-to-all-start) | async-done | bytes 131104 | tf_op jit(solution)/shard_map/all_to_all | solution.py:376
  15.6 0.7 %shard_map.88 = f32[8,24,128]{2,1,0:T(8,128)} custom-call(bf16[32,16,128]{2,1,0:T(8,128)(2,1)S(1)} %all-to-all-done.got, f32[8,128]{1,0:T(8,128)S(1)} %shard_map.87.z_both), custom_call_target="tpu_custom_call" | custom-call | flops 1000000 | bytes 200000 | tf_op jit(solution)/shard_map/pallas_call | solution.py:335
  16.2 10.1 %all-to-all-start.1 = ((f32[8,24,128]{2,1,0:T(8,128)}), f32[8,24,128]{2,1,0:T(8,128)S(1)}, u32[]{:S(2)}, u32[]{:S(2)}) async-start(f32[8,24,128]{2,1,0:T(8,128)} %shard_map.88), calls=%async_computation.1 | async-start | bytes 196608 | tf_op jit(solution)/shard_map/all_to_all | solution.py:392
  26.4 2.6 %collective-permute-start = (f32[5,5,160]{2,1,0:T(8,128)}, f32[5,5,160]{2,1,0:T(8,128)S(1)}, u32[]{:S(2)}, u32[]{:S(2)}) collective-permute-start(f32[5,5,160]{2,1,0:T(8,128)} %get-tuple-element.10), channel_id=1, source_target_pairs={{0,32},{32,64},{64,96},{96,128},{128,160},{160,192},{192,224},{224... | collective-permute-start | bytes 48008 | tf_op jit(solution)/shard_map/ppermute | solution.py:384
  29.0 2.4 %collective-permute-start.1 = (f32[5,5,160]{2,1,0:T(8,128)}, f32[5,5,160]{2,1,0:T(8,128)S(1)}, u32[]{:S(2)}, u32[]{:S(2)}) collective-permute-start(f32[5,5,160]{2,1,0:T(8,128)} %get-tuple-element.11), channel_id=1, source_target_pairs={{0,224},{32,0},{64,32},{96,64},{128,96},{160,128},{192,160},{224,1... | collective-permute-start | bytes 48008 | tf_op jit(solution)/shard_map/ppermute | solution.py:384
  31.4 2.4 %collective-permute-start.2 = (f32[5,5,160]{2,1,0:T(8,128)}, f32[5,5,160]{2,1,0:T(8,128)S(1)}, u32[]{:S(2)}, u32[]{:S(2)}) collective-permute-start(f32[5,5,160]{2,1,0:T(8,128)} %get-tuple-element.12), channel_id=1, source_target_pairs={{0,8},{8,16},{16,24},{24,0},{1,9},{9,17},{17,25},{25,1},{2,10},{10... | collective-permute-start | bytes 48008 | tf_op jit(solution)/shard_map/ppermute | solution.py:384
  33.9 0.0 collective-permute-start.3
  33.9 0.0 copy-start
  33.9 1.3 %copy-done = bf16[4,320,512]{2,1,0:T(8,128)(2,1)S(1)} copy-done((bf16[4,320,512]{2,1,0:T(8,128)(2,1)S(1)}, bf16[4,320,512]{2,1,0:T(8,128)(2,1)}, u32[]{:S(2)}) %copy-start) | copy-done | bytes 1310744
  35.2 0.1 shard_map.90.weights
  35.3 0.0 copy-start.1
  35.3 0.0 copy-start.3
  35.3 0.0 all-to-all-done.1.z_all.got
  35.3 1.0 %shard_map.91 = f32[32,1,16]{2,1,0:T(1,128)} custom-call(f32[8,24,128]{2,1,0:T(8,128)S(1)} %all-to-all-done.1.z_all.got, bf16[4,320,512]{2,1,0:T(8,128)(2,1)S(1)} %shard_map.90.weights), custom_call_target="tpu_custom_call" | custom-call | flops 1000000 | bytes 200000 | tf_op jit(solution)/shard_map/pallas_call | solution.py:335
  36.3 5.9 %all-to-all-start.2 = ((f32[32,1,16]{2,1,0:T(1,128)}), f32[32,1,16]{2,1,0:T(1,128)S(1)}, u32[]{:S(2)}, u32[]{:S(2)}) async-start(f32[32,1,16]{2,1,0:T(1,128)} %shard_map.91), calls=%async_computation.2 | async-start | bytes 32768 | tf_op jit(solution)/shard_map/all_to_all | solution.py:394
  42.2 0.0 collective-permute-done.x_low
  42.2 0.0 collective-permute-done.1.x_up
  42.2 0.0 collective-permute-done.2.y_low
  42.2 0.0 collective-permute-done.3.y_up
  42.2 0.0 copy-done.1
  42.2 0.0 copy-done.3
  42.3 2.3 %shard_map.89 = f32[5,5,5,160]{3,2,1,0:T(8,128)} custom-call(f32[5,5,8,256]{3,2,1,0:T(8,128)S(1)} %copy-done.1, f32[1,32]{1,0:T(1,128)S(1)} %bitcast.5, f32[5,5,160]{2,1,0:T(8,128)S(1)} %collective-permute-done.x_low, f32[5,5,160]{2,1,0:T(8,128)S(1)} %collective-permute-done.1.x_up, f32[5,5,160]{2,1,0:T(8,128)S(1)} %collective-permute-done.2.y_low, ...), custom_call_target="tpu_custom_call" | custom-call | flops 20000000 | bytes 200000 | tf_op jit(solution)/shard_map/pallas_call | solution.py:335
  44.6 2.0 %all-to-all-done.2.tiles = f32[32,1,16]{2,1,0:T(1,128)S(1)} async-done(((f32[32,1,16]{2,1,0:T(1,128)}), f32[32,1,16]{2,1,0:T(1,128)S(1)}, u32[]{:S(2)}, u32[]{:S(2)}) %all-to-all-start.2) | async-done | bytes 2080 | tf_op jit(solution)/shard_map/all_to_all | solution.py:394
  46.6 0.5 %shard_map.92 = f32[1,16]{1,0:T(1,128)} custom-call(f32[32,1,16]{2,1,0:T(1,128)S(1)} %all-to-all-done.2.tiles), custom_call_target="tpu_custom_call" | custom-call | flops 1000000 | bytes 200000 | tf_op jit(solution)/shard_map/pallas_call | solution.py:335
  (1 shorter events, 0.0 us)
Async XLA Ops:
  2.9 12.7 %all-to-all-start = ((bf16[32,16,128]{2,1,0:T(8,128)(2,1)}), bf16[32,16,128]{2,1,0:T(8,128)(2,1)S(1)}, u32[]{:S(2)}, u32[]{:S(2)}) async-start(bf16[32,16,128]{2,1,0:T(8,128)(2,1)} %get-tuple-element.14), calls=%async_computation | async-start | bytes 262144 | tf_op jit(solution)/shard_map/all_to_all | solution.py:376
  12.8 0.7 %copy-start.2 = (f32[8,128]{1,0:T(8,128)S(1)}, f32[8,128]{1,0:T(8,128)}, u32[]{:S(2)}) copy-start(f32[8,128]{1,0:T(8,128)} %get-tuple-element.15.array) | copy-start | bytes 12292
  16.2 19.1 %all-to-all-start.1 = ((f32[8,24,128]{2,1,0:T(8,128)}), f32[8,24,128]{2,1,0:T(8,128)S(1)}, u32[]{:S(2)}, u32[]{:S(2)}) async-start(f32[8,24,128]{2,1,0:T(8,128)} %shard_map.88), calls=%async_computation.1 | async-start | bytes 196608 | tf_op jit(solution)/shard_map/all_to_all | solution.py:392
  26.4 15.8 %collective-permute-start = (f32[5,5,160]{2,1,0:T(8,128)}, f32[5,5,160]{2,1,0:T(8,128)S(1)}, u32[]{:S(2)}, u32[]{:S(2)}) collective-permute-start(f32[5,5,160]{2,1,0:T(8,128)} %get-tuple-element.10), channel_id=1, source_target_pairs={{0,32},{32,64},{64,96},{96,128},{128,160},{160,192},{192,224},{224... | collective-permute-start | bytes 48008 | tf_op jit(solution)/shard_map/ppermute | solution.py:384
  29.0 13.2 %collective-permute-start.1 = (f32[5,5,160]{2,1,0:T(8,128)}, f32[5,5,160]{2,1,0:T(8,128)S(1)}, u32[]{:S(2)}, u32[]{:S(2)}) collective-permute-start(f32[5,5,160]{2,1,0:T(8,128)} %get-tuple-element.11), channel_id=1, source_target_pairs={{0,224},{32,0},{64,32},{96,64},{128,96},{160,128},{192,160},{224,1... | collective-permute-start | bytes 48008 | tf_op jit(solution)/shard_map/ppermute | solution.py:384
  31.4 10.8 %collective-permute-start.2 = (f32[5,5,160]{2,1,0:T(8,128)}, f32[5,5,160]{2,1,0:T(8,128)S(1)}, u32[]{:S(2)}, u32[]{:S(2)}) collective-permute-start(f32[5,5,160]{2,1,0:T(8,128)} %get-tuple-element.12), channel_id=1, source_target_pairs={{0,8},{8,16},{16,24},{24,0},{1,9},{9,17},{17,25},{25,1},{2,10},{10... | collective-permute-start | bytes 48008 | tf_op jit(solution)/shard_map/ppermute | solution.py:384
  33.9 8.4 %collective-permute-start.3 = (f32[5,5,160]{2,1,0:T(8,128)}, f32[5,5,160]{2,1,0:T(8,128)S(1)}, u32[]{:S(2)}, u32[]{:S(2)}) collective-permute-start(f32[5,5,160]{2,1,0:T(8,128)} %get-tuple-element.13), channel_id=1, source_target_pairs={{0,24},{8,0},{16,8},{24,16},{1,25},{9,1},{17,9},{25,17},{2,26},{10... | collective-permute-start | bytes 48008 | tf_op jit(solution)/shard_map/ppermute | solution.py:384
  33.9 1.3 %copy-start = (bf16[4,320,512]{2,1,0:T(8,128)(2,1)S(1)}, bf16[4,320,512]{2,1,0:T(8,128)(2,1)}, u32[]{:S(2)}) copy-start(bf16[4,320,512]{2,1,0:T(8,128)(2,1)} %array.1) | copy-start | bytes 3932164
  35.3 7.0 %copy-start.1 = (f32[5,5,8,256]{3,2,1,0:T(8,128)S(1)}, f32[5,5,8,256]{3,2,1,0:T(8,128)}, u32[]{:S(2)}) copy-start(f32[5,5,8,256]{3,2,1,0:T(8,128)} %get-tuple-element.9.start) | copy-start | bytes 614404
  35.3 7.0 %copy-start.3 = (f32[1,1,32]{2,1,0:T(1,128)S(1)}, f32[1,1,32]{2,1,0:T(1,128)}, u32[]{:S(2)}) copy-start(f32[1,1,32]{2,1,0:T(1,128)} %param.10) | copy-start | bytes 388
  36.3 10.3 %all-to-all-start.2 = ((f32[32,1,16]{2,1,0:T(1,128)}), f32[32,1,16]{2,1,0:T(1,128)S(1)}, u32[]{:S(2)}, u32[]{:S(2)}) async-start(f32[32,1,16]{2,1,0:T(1,128)} %shard_map.91), calls=%async_computation.2 | async-start | bytes 32768 | tf_op jit(solution)/shard_map/all_to_all | solution.py:394

commit v2 on v1

--- a/solution.py
+++ b/solution.py
@@ -16,6 +16,9 @@
 PLACE_FIRST = 21
 SHARE_FIRST = 4
 COLLECT_FIRST = 17
+Z_ROWS = 10
+HINT_FLOPS = 20_000_000_000
+HINT_BYTES = 800_000_000
 
 
 def rotated(count, first):
@@ -77,19 +80,12 @@
                 grid[1 + m, x, y : y + 1, 0:nz] = vel[x, y, m : m + 1, :]
 
 
-def face_kernel(per_group, den, vel, pre, sid, code, blocks, x_lo, x_hi, y_lo, y_hi, z_both, grid, rows, den_v, vel_v, pre_v, sid_v, code_v, sems):
-    pairs = ((den, den_v), (vel, vel_v), (pre, pre_v), (sid, sid_v), (code, code_v))
-    loads = [pltpu.make_async_copy(src, dst, sems.at[i]) for i, (src, dst) in enumerate(pairs)]
-    for load in loads:
-        load.start()
+def face_kernel(per_group, mask, den, vel, pre, sid, code, blocks, x_lo, x_hi, y_lo, y_hi, z_both, grid, rows):
     nx, ny, nz = den.shape
     slots = sid.shape[1]
     groups = blocks.shape[0]
     rows[...] = jnp.zeros_like(rows)
-    for load in loads:
-        load.wait()
-
-    lay_out(den_v, vel_v, pre_v, grid)
+    lay_out(den, vel, pre, grid)
 
     def field(f, x):
         return grid[f, x, 0:ny, 0:nz]
@@ -117,8 +113,8 @@
         rows[8 * q + 4 : 8 * q + 5, :] = -over_z
         rows[8 * q + 5 : 8 * q + 6, :] = over_z
 
-    face = lax.shift_right_logical(code_v[...], 5)
-    elem = code_v[...] & 31
+    face = lax.shift_right_logical(code[...], 5)
+    elem = code[...] & 31
     z = iota((nz, slots), 0)
     z_elem = lax.shift_right_logical(z * 52429, 18)
     z_node = z - 5 * z_elem
@@ -131,22 +127,24 @@
         for q in range(4)
     ]
 
-    ids = sid_v[...]
+    ids = sid[...]
     group = lax.shift_right_logical(jnp.maximum(ids, 0) * 6554, 21)
     offset = ids - per_group * group
-    chunk = lax.shift_right_logical(jnp.maximum(offset, 0), 7)
     group = jnp.where(ids >= 0, (group + groups - PLACE_FIRST) & (groups - 1), -1)
     row = iota((16, slots), 0)
-    row_q = lax.shift_right_logical(row * 21846, 16)
-    spread = jnp.zeros((16, slots), F32)
-    for q in range(4):
-        spread = jnp.where(row_q == q, data[q], spread)
-    spread = jnp.where(row - 3 * row_q == chunk, spread, F32(0)).astype(BF16).astype(F32)
     group_of = iota((groups, 16, slots), 0)
-    spread = jnp.where(group_of == group[None], spread[None], F32(0))
-    spread = spread.reshape(groups * 16, slots).astype(BF16)
-    lane_hot = (iota((128, slots), 0) == (offset & 127)).astype(F32).astype(BF16)
-    placed = lax.dot_general(spread, lane_hot, (((1,), (1,)), ((), ())), preferred_element_type=F32)
+    placed = jnp.zeros((groups * 16, 128), F32)
+    for shift in sorted({q * per_group % 128 for q in range(4)}):
+        spread = jnp.zeros((16, slots), F32)
+        for q in range(4):
+            if q * per_group % 128 == shift:
+                at = lax.shift_right_logical(jnp.maximum(q * per_group + offset, 0), 7)
+                spread = jnp.where(row == at, data[q], spread)
+        spread = spread.astype(BF16).astype(F32)
+        spread = jnp.where(group_of == group[None], spread[None], F32(0))
+        spread = spread.reshape(groups * 16, slots).astype(BF16)
+        lane_hot = (iota((128, slots), 0) == ((shift + offset) & 127)).astype(F32).astype(BF16)
+        placed += lax.dot_general(spread, lane_hot, (((1,), (1,)), ((), ())), preferred_element_type=F32)
     blocks[...] = placed.astype(BF16).reshape(groups, 16, 128)
 
     for f in range(5):
@@ -156,15 +154,22 @@
             y_lo[f, x : x + 1] = grid[f, x, 0:1, 0:nz]
             y_hi[f, x : x + 1] = grid[f, x, ny - 1 : ny, 0:nz]
 
-    z_both[...] = jnp.zeros_like(z_both)
-    packed = jnp.zeros((ny, 128), F32)
+    z_both[...] = F32(1) - mask[...]
+    z_both[0:Z_ROWS] = jnp.zeros((Z_ROWS, 128), F32)
     lane = iota((ny, 128), 1)
-    for f in range(5):
-        for x in range(nx):
-            at = 5 * f + x
-            packed = jnp.where(lane == at, grid[f, x, 0:ny, 0:1], packed)
-            packed = jnp.where(lane == 64 + at, grid[f, x, 0:ny, nz - 1 : nz], packed)
-    z_both[0:ny] = packed
+    for side, node in enumerate((0, nz - 1)):
+        packed = jnp.zeros((ny, 128), F32)
+        for f in range(5):
+            for x in range(nx):
+                packed = jnp.where(lane == nx * f + x, grid[f, x, 0:ny, node : node + 1], packed)
+        rows[0:ny, 0:128] = packed
+        rest = rows[0:1, 0:128]
+        for y in range(1, ny):
+            rest = rest + pltpu.roll(jnp.broadcast_to(rows[y : y + 1, 0:128], (8, 128)), 5 * nx * y, 1)[0:1]
+        for part in range(3):
+            rounded = rest.astype(BF16).astype(F32)
+            z_both[Z_ROWS + 3 * side + part : Z_ROWS + 3 * side + part + 1] = rounded
+            rest = rest - rounded
 
 
 def split_flux(a, b, d):
@@ -209,9 +214,20 @@
     grid[...] = jnp.ones_like(grid)
     layers = z_all.shape[0]
     here = lax.axis_index("gz")
-    at = here + 2 * layers - SHARE_FIRST
-    z_low = z_all[lax.rem(at - 1, layers), 16:24]
-    z_up = z_all[lax.rem(at + 1, layers), 16:24]
+
+    def from_layer(step, side):
+        at = lax.rem(here + 2 * layers - SHARE_FIRST + step, layers)
+        parts = z_all[at].astype(F32)
+        first = Z_ROWS + 3 * side
+        line = (parts[first + 2 : first + 3] + parts[first + 1 : first + 2]) + parts[first : first + 1]
+        line = jnp.broadcast_to(line, (8, 128))
+        found = line
+        for y in range(1, ny):
+            found = jnp.where(iota((8, 128), 0) == y, pltpu.roll(line, 128 - 5 * nx * y, 1), found)
+        return found
+
+    z_low = from_layer(-1, 1)
+    z_up = from_layer(1, 0)
     half_lane = iota((8, 128), 1)
     outside = (iota((8, 128), 0) >= ny) & (half_lane >= nz - 128)
     for f in range(5):
@@ -224,7 +240,7 @@
             at = 5 * f + x
             upper = grid[f, 1 + x, :, 128:256]
             upper = jnp.where(half_lane == nz - 128, pltpu.roll(z_up, (nz - 128 - at) % 128, 1), upper)
-            upper = jnp.where(half_lane == 127, pltpu.roll(z_low, (127 - 64 - at) % 128, 1), upper)
+            upper = jnp.where(half_lane == 127, pltpu.roll(z_low, (127 - at) % 128, 1), upper)
             upper = jnp.where(outside, F32(1), upper)
             grid[f, 1 + x, :, 128:256] = upper
 
@@ -295,27 +311,33 @@
 
 
 def gather_kernel(got, z_both, copies):
-    total = got[0].astype(F32)
+    total = z_both[...]
+    for i in range(got.shape[0]):
+        total = total + got[i].astype(F32)
+    total = total.astype(BF16)
+    for i in range(copies.shape[0]):
+        copies[i] = total
+
+
+def mask_kernel(mask):
+    mask[...] = jnp.where(iota(mask.shape, 0) >= Z_ROWS, F32(1), F32(0))
+
+
+def signal_kernel(got, weights, out):
+    data = got[0].astype(F32)
     for i in range(1, got.shape[0]):
-        total = total + got[i].astype(F32)
-    for i in range(copies.shape[0]):
-        copies[i, 0:16] = total
-        copies[i, 16:24] = z_both[...]
-
-
-def keep_kernel(array, kept):
-    kept[...] = array[...]
-
-
-def signal_kernel(got, weights, out):
-    blocks = jnp.zeros((got.shape[0], weights.shape[2]), F32)
+        data = data + got[i].astype(F32)
+    data = data.astype(BF16)
+    total = jnp.zeros((1, weights.shape[2]), F32)
     faces = weights.shape[1]
     for q in range(weights.shape[0]):
-        for c in range(3):
-            width = min(128, faces - 128 * c)
-            data = got[:, 3 * q + c, 0:width].astype(BF16)
-            blocks = blocks + jnp.dot(data, weights[q, 128 * c : 128 * c + width, :], preferred_element_type=F32)
-    total = jnp.sum(blocks, axis=0, keepdims=True)
+        face = 0
+        while face < faces:
+            row, lane = divmod(q * faces + face, 128)
+            width = min(128 - lane, faces - face)
+            part = data[row : row + 1, lane : lane + width]
+            total = total + jnp.dot(part, weights[q, face : face + width, :], preferred_element_type=F32)
+            face += width
     size = out.shape[2]
     for g in range(out.shape[0]):
         at = (g + COLLECT_FIRST) % out.shape[0]
@@ -329,7 +351,7 @@
     out[...] = total
 
 
-def call(kernel, outs, args, scratch=(), flops=1_000_000, hbm=(), limit=16, aliases=None):
+def call(kernel, outs, args, scratch=(), flops=1_000_000, hbm=(), limit=16, aliases=None, moved=200_000):
     single = not isinstance(outs, (list, tuple))
     inside = pl.BlockSpec(memory_space=pltpu.VMEM)
     return pl.pallas_call(
@@ -340,7 +362,7 @@
         scratch_shapes=scratch,
         input_output_aliases=aliases or {},
         compiler_params=pltpu.CompilerParams(vmem_limit_bytes=limit * 1024 * 1024),
-        cost_estimate=pl.CostEstimate(flops=flops, bytes_accessed=200_000, transcendentals=0),
+        cost_estimate=pl.CostEstimate(flops=flops, bytes_accessed=moved, transcendentals=0),
     )(*args)
 
 
@@ -352,32 +374,20 @@
     _, faces, local = face_signal_weights.shape
     ids = surf_id.reshape(1, -1)
     codes = surface_face_code.reshape(1, -1)
-    slots = ids.shape[1]
     speeds = jnp.transpose(velocity, (1, 2, 0, 3))
+    mask = call(mask_kernel, sds((16, 128), F32), [], flops=HINT_FLOPS, moved=HINT_BYTES)
     blocks, x_lo, x_hi, y_lo, y_hi, z_both, grid = call(
         functools.partial(face_kernel, faces),
         [sds((groups, 16, 128), BF16)]
         + [sds((5, ny, nz), F32)] * 2
         + [sds((5, nx, nz), F32)] * 2
-        + [sds((8, 128), F32), sds((5, nx, 8, LANES), F32)],
-        [density, speeds, pressure, ids, codes],
+        + [sds((16, 128), F32), sds((5, nx, 8, LANES), F32)],
+        [mask, density, speeds, pressure, ids, codes],
         [
             pltpu.VMEM((32, nz), F32),
-            pltpu.VMEM((nx, ny, nz), F32),
-            pltpu.VMEM((nx, ny, 3, nz), F32),
-            pltpu.VMEM((nx, ny, nz), F32),
-            pltpu.VMEM((1, slots), jnp.int32),
-            pltpu.VMEM((1, slots), jnp.int32),
-            pltpu.SemaphoreType.DMA((5,)),
         ],
-        hbm=(0, 1, 2, 3, 4),
-        limit=60,
     )
     arrived = lax.all_to_all(blocks, PAIR, 0, 0, tiled=True, axis_index_groups=[rotated(groups, PLACE_FIRST)])
-    held = call(
-        keep_kernel, sds(face_signal_weights.shape, BF16), [face_signal_weights], flops=2_000_000
-    )
-    z_kept = call(keep_kernel, sds(z_both.shape, F32), [z_both])
 
     def shift(array, axis, step):
         peers = lax.axis_size(axis)
@@ -388,9 +398,9 @@
     y_low = shift(y_hi, "gy", 1)
     y_up = shift(y_lo, "gy", -1)
 
-    copies = call(gather_kernel, sds((layers, 24, 128), F32), [arrived, z_kept])
+    copies = call(gather_kernel, sds((layers, 16, 128), BF16), [arrived, z_both], flops=HINT_FLOPS, moved=HINT_BYTES)
     everywhere = lax.all_to_all(copies, "gz", 0, 0, tiled=True, axis_index_groups=[rotated(layers, SHARE_FIRST)])
-    partial = call(signal_kernel, sds((groups, 1, local // groups), F32), [everywhere, held])
+    partial = call(signal_kernel, sds((groups, 1, local // groups), F32), [everywhere, face_signal_weights])
     tiles = lax.all_to_all(partial, PAIR, 0, 0, tiled=True, axis_index_groups=[rotated(groups, COLLECT_FIRST)])
     signals = call(sum_kernel, sds((1, local // groups), F32), [tiles]).reshape(-1)
 

time: 47.5 us -> 45.2 us (0.952)
  blocking collectives: 0 us -> 12.5 us
  starting transfers between devices: 33.4 us -> 23.6 us
  waiting for transfers between devices: 4.11 us -> 2.01 us
  Pallas kernels: 6.86 us -> 5.23 us
  local copies, waits for them, and re-layouts: 2 us -> 0.91 us
    all_to_all x0 -> x1, blocking collectives: none -> 12.5 us  [step(): lax.all_to_all(blocks, PAIR, 0, 0, tiled=True, axis_index_groups=[rotated...]
    all_to_all x1 -> x0, starting transfers between devices: 9.9 us -> none  [step(): lax.all_to_all(blocks, PAIR, 0, 0, tiled=True, axis_index_groups=[rotated...]
    all_to_all x1 -> x0, waiting for transfers between devices: 2.12 us -> none  [step(): lax.all_to_all(blocks, PAIR, 0, 0, tiled=True, axis_index_groups=[rotated...]
    pallas_call x7 -> x6, Pallas kernels: 6.86 us -> 5.23 us  [call(): pl.pallas_call(kernel, out_shape=outs, in_specs=[pl.BlockSpec(memory_spac...]
    unnamed x8 -> x14, local copies, waits for them, and re-layouts: 2 us -> 0.91 us
  transfers between devices with their start and end apart: 7 -> 6, of which waited for: 2 -> 1; matrix products, arithmetic and copies ran while one was open for 0% -> 0% of each run, Pallas kernels for 7% -> 7%
where the time goes in v2:
time: 45.2 us; the launch traced here: 45 us
  starting transfers between devices  23.6 us (52%)
  blocking collectives  12.5 us (28%)
  Pallas kernels  5.23 us (12%)
  waiting for transfers between devices  2.01 us (4%)
  local copies, waits for them, and re-layouts  0.91 us (2%)
  between operations  0.74 us (2%)
    all_to_all x1, blocking collectives, step(): lax.all_to_all(blocks, PAIR, 0, 0, tiled=True, axis_index_groups=[rotated...  12.5 us
    all_to_all x1, starting transfers between devices, step(): lax.all_to_all(copies, 'gz', 0, 0, tiled=True, axis_index_groups=[rotated...  10.2 us
    ppermute x4, starting transfers between devices, shift(): lax.ppermute(array, axis, [(i, (i + step) % peers) for i in range(peers)])  7.5 us
    all_to_all x1, starting transfers between devices, step(): lax.all_to_all(partial, PAIR, 0, 0, tiled=True, axis_index_groups=[rotate...  5.86 us
    pallas_call x6, Pallas kernels, call(): pl.pallas_call(kernel, out_shape=outs, in_specs=[pl.BlockSpec(memory_spac...  5.23 us
    all_to_all x1, waiting for transfers between devices, step(): lax.all_to_all(partial, PAIR, 0, 0, tiled=True, axis_index_groups=[rotate...  1.99 us
    unnamed x14, local copies, waits for them, and re-layouts  0.91 us
  transfers between devices with their start and end apart: 6, of which 1 were waited for; matrix products, arithmetic and copies ran while one was open for 0% of the time, Pallas kernels for 7%

profile of v2, /device:TPU:1, one launch (start us, length us, event | category | flops | bytes accessed | tf_op | source)
XLA Modules:
  0.0 45.0 jit_solution(14366295793905237888)
XLA Ops:
  0.6 0.0 copy-start.5
  0.6 0.0 copy-start.4
  0.7 0.0 copy-start.3
  0.7 0.0 copy-start.1
  0.7 0.0 copy-start.2
  0.7 0.6 %copy-done.5 = s32[120]{0:T(128)S(1)} copy-done((s32[120]{0:T(128)S(1)}, s32[120]{0:T(128)}, u32[]{:S(2)}) %copy-start.5) | copy-done | bytes 504
  1.3 0.0 copy-done.4
  1.3 0.1 copy-done.3
  1.4 0.1 copy-done.1
  1.6 0.0 copy-done.2
  1.6 0.7 %shard_map.87 = (bf16[32,16,128]{2,1,0:T(8,128)(2,1)S(1)}, f32[5,5,160]{2,1,0:T(8,128)S(1)}, f32[5,5,160]{2,1,0:T(8,128)S(1)}, f32[5,5,160]{2,1,0:T(8,128)S(1)},...) custom-call(f32[16,128]{1,0:T(8,128)S(1)} %shard_map.86.mask, ...), custom_call_target="tpu_custom_call" | custom-call | flops 1000000 | bytes 200000 | tf_op jit(solution)/shard_map/pallas_call | solution.py:357
  2.3 12.5 %all_to_all.15.got = bf16[32,16,128]{2,1,0:T(8,128)(2,1)S(1)} all-to-all(bf16[32,16,128]{2,1,0:T(8,128)(2,1)S(1)} %get-tuple-element.14), channel_id=1, replica_groups={{168,176,184,192,200,208,216,224,232,240,248,0,8,16,24,32,40,48,56,64,7..., dimensions={0} | all-to-all | bytes 262144 | tf_op jit(solution)/shard_map/all_to_all | solution.py:390
  14.8 0.0 copy-start
  14.8 0.7 %shard_map.88 = bf16[8,16,128]{2,1,0:T(8,128)(2,1)} custom-call(bf16[32,16,128]{2,1,0:T(8,128)(2,1)S(1)} %all_to_all.15.got, f32[16,128]{1,0:T(8,128)S(1)} %get-tuple-element.15.z_both), custom_call_target="tpu_custom_call" | custom-call | flops 20000000000 | bytes 800000000 | tf_op jit(solution)/shard_map/pallas_call | solution.py:357
  15.4 0.0 copy-start.6
  15.4 10.2 %all-to-all-start.1 = ((bf16[8,16,128]{2,1,0:T(8,128)(2,1)}), bf16[8,16,128]{2,1,0:T(8,128)(2,1)S(1)}, u32[]{:S(2)}, u32[]{:S(2)}) async-start(bf16[8,16,128]{2,1,0:T(8,128)(2,1)} %shard_map.88), calls=%async_computation.1 | async-start | bytes 65536 | tf_op jit(solution)/shard_map/all_to_all | solution.py:402
  25.7 2.6 %collective-permute-start = (f32[5,5,160]{2,1,0:T(8,128)S(1)}, f32[5,5,160]{2,1,0:T(8,128)S(1)}, u32[]{:S(2)}, u32[]{:S(2)}) collective-permute-start(f32[5,5,160]{2,1,0:T(8,128)S(1)} %get-tuple-element.10), channel_id=1, source_target_pairs={{0,32},{32,64},{64,96},{96,128},{128,160},{160,192},{192,224},{224... | collective-permute-start | bytes 48008 | tf_op jit(solution)/shard_map/ppermute | solution.py:394
  28.3 2.4 %collective-permute-start.1 = (f32[5,5,160]{2,1,0:T(8,128)S(1)}, f32[5,5,160]{2,1,0:T(8,128)S(1)}, u32[]{:S(2)}, u32[]{:S(2)}) collective-permute-start(f32[5,5,160]{2,1,0:T(8,128)S(1)} %get-tuple-element.11), channel_id=1, source_target_pairs={{0,224},{32,0},{64,32},{96,64},{128,96},{160,128},{192,160},{224,1... | collective-permute-start | bytes 48008 | tf_op jit(solution)/shard_map/ppermute | solution.py:394
  30.7 2.4 %collective-permute-start.2 = (f32[5,5,160]{2,1,0:T(8,128)S(1)}, f32[5,5,160]{2,1,0:T(8,128)S(1)}, u32[]{:S(2)}, u32[]{:S(2)}) collective-permute-start(f32[5,5,160]{2,1,0:T(8,128)S(1)} %get-tuple-element.12), channel_id=1, source_target_pairs={{0,8},{8,16},{16,24},{24,0},{1,9},{9,17},{17,25},{25,1},{2,10},{10... | collective-permute-start | bytes 48008 | tf_op jit(solution)/shard_map/ppermute | solution.py:394
  33.2 0.0 collective-permute-start.3
  33.2 0.0 all-to-all-done.1.z_all.got
  33.2 0.0 copy-done
  33.2 1.0 %shard_map.90 = f32[32,1,16]{2,1,0:T(1,128)} custom-call(bf16[8,16,128]{2,1,0:T(8,128)(2,1)S(1)} %all-to-all-done.1.z_all.got, bf16[4,320,512]{2,1,0:T(8,128)(2,1)S(1)} %copy-done), custom_call_target="tpu_custom_call" | custom-call | flops 1000000 | bytes 200000 | tf_op jit(solution)/shard_map/pallas_call | solution.py:357
  34.2 5.9 %all-to-all-start.2 = ((f32[32,1,16]{2,1,0:T(1,128)}), f32[32,1,16]{2,1,0:T(1,128)S(1)}, u32[]{:S(2)}, u32[]{:S(2)}) async-start(f32[32,1,16]{2,1,0:T(1,128)} %shard_map.90), calls=%async_computation.2 | async-start | bytes 32768 | tf_op jit(solution)/shard_map/all_to_all | solution.py:404
  40.1 0.0 collective-permute-done.x_low
  40.1 0.0 collective-permute-done.1.x_up
  40.1 0.0 collective-permute-done.2.y_low
  40.1 0.0 collective-permute-done.3.y_up
  40.1 0.0 copy-done.6
  40.1 2.3 %shard_map.89 = f32[5,5,5,160]{3,2,1,0:T(8,128)} custom-call(f32[5,5,8,256]{3,2,1,0:T(8,128)S(1)} %get-tuple-element.9.start, f32[1,32]{1,0:T(1,128)S(1)} %bitcast.8, f32[5,5,160]{2,1,0:T(8,128)S(1)} %collective-permute-done.x_low, f32[5,5,160]{2,1,0:T(8,128)S(1)} %collective-permute-done.1.x_up, f32[5,5,160]{2,1,0:T(8,128)S(1)} %collective-permute-done.2.y_low, ...), custom_call_target="tpu_custom_call" | custom-call | flops 20000000 | bytes 200000 | tf_op jit(solution)/shard_map/pallas_call | solution.py:357
  42.4 2.0 %all-to-all-done.2.tiles = f32[32,1,16]{2,1,0:T(1,128)S(1)} async-done(((f32[32,1,16]{2,1,0:T(1,128)}), f32[32,1,16]{2,1,0:T(1,128)S(1)}, u32[]{:S(2)}, u32[]{:S(2)}) %all-to-all-start.2) | async-done | bytes 2080 | tf_op jit(solution)/shard_map/all_to_all | solution.py:404
  44.4 0.5 %shard_map.91 = f32[1,16]{1,0:T(1,128)} custom-call(f32[32,1,16]{2,1,0:T(1,128)S(1)} %all-to-all-done.2.tiles), custom_call_target="tpu_custom_call" | custom-call | flops 1000000 | bytes 200000 | tf_op jit(solution)/shard_map/pallas_call | solution.py:357
  (1 shorter events, 0.0 us)
Async XLA Ops:
  0.6 0.7 %copy-start.5 = (s32[120]{0:T(128)S(1)}, s32[120]{0:T(128)}, u32[]{:S(2)}) copy-start(s32[120]{0:T(128)} %param.13) | copy-start | bytes 1444
  0.6 0.7 %copy-start.4 = (s32[120]{0:T(128)S(1)}, s32[120]{0:T(128)}, u32[]{:S(2)}) copy-start(s32[120]{0:T(128)} %param.12) | copy-start | bytes 1444
  0.7 0.8 %copy-start.3 = (f32[5,5,160]{2,1,0:T(8,128)S(1)}, f32[5,5,160]{2,1,0:T(8,128)}, u32[]{:S(2)}) copy-start(f32[5,5,160]{2,1,0:T(8,128)} %pre.1) | copy-start | bytes 48004
  0.7 0.9 %copy-start.1 = (f32[3,5,5,160]{3,0,2,1:T(4,128)S(1)}, f32[3,5,5,160]{3,0,2,1:T(4,128)}, u32[]{:S(2)}) copy-start(f32[3,5,5,160]{3,0,2,1:T(4,128)} %param.8) | copy-start | bytes 144004
  0.7 0.9 %copy-start.2 = (f32[5,5,160]{2,1,0:T(8,128)S(1)}, f32[5,5,160]{2,1,0:T(8,128)}, u32[]{:S(2)}) copy-start(f32[5,5,160]{2,1,0:T(8,128)} %den.1) | copy-start | bytes 48004
  14.8 18.4 %copy-start = (bf16[4,320,512]{2,1,0:T(8,128)(2,1)S(1)}, bf16[4,320,512]{2,1,0:T(8,128)(2,1)}, u32[]{:S(2)}) copy-start(bf16[4,320,512]{2,1,0:T(8,128)(2,1)} %weights.1) | copy-start | bytes 3932164
  15.4 24.7 %copy-start.6 = (f32[1,1,32]{2,1,0:T(1,128)S(1)}, f32[1,1,32]{2,1,0:T(1,128)}, u32[]{:S(2)}) copy-start(f32[1,1,32]{2,1,0:T(1,128)} %param.10) | copy-start | bytes 388
  15.4 17.7 %all-to-all-start.1 = ((bf16[8,16,128]{2,1,0:T(8,128)(2,1)}), bf16[8,16,128]{2,1,0:T(8,128)(2,1)S(1)}, u32[]{:S(2)}, u32[]{:S(2)}) async-start(bf16[8,16,128]{2,1,0:T(8,128)(2,1)} %shard_map.88), calls=%async_computation.1 | async-start | bytes 65536 | tf_op jit(solution)/shard_map/all_to_all | solution.py:402
  25.7 14.4 %collective-permute-start = (f32[5,5,160]{2,1,0:T(8,128)S(1)}, f32[5,5,160]{2,1,0:T(8,128)S(1)}, u32[]{:S(2)}, u32[]{:S(2)}) collective-permute-start(f32[5,5,160]{2,1,0:T(8,128)S(1)} %get-tuple-element.10), channel_id=1, source_target_pairs={{0,32},{32,64},{64,96},{96,128},{128,160},{160,192},{192,224},{224... | collective-permute-start | bytes 48008 | tf_op jit(solution)/shard_map/ppermute | solution.py:394
  28.3 11.8 %collective-permute-start.1 = (f32[5,5,160]{2,1,0:T(8,128)S(1)}, f32[5,5,160]{2,1,0:T(8,128)S(1)}, u32[]{:S(2)}, u32[]{:S(2)}) collective-permute-start(f32[5,5,160]{2,1,0:T(8,128)S(1)} %get-tuple-element.11), channel_id=1, source_target_pairs={{0,224},{32,0},{64,32},{96,64},{128,96},{160,128},{192,160},{224,1... | collective-permute-start | bytes 48008 | tf_op jit(solution)/shard_map/ppermute | solution.py:394
  30.7 9.3 %collective-permute-start.2 = (f32[5,5,160]{2,1,0:T(8,128)S(1)}, f32[5,5,160]{2,1,0:T(8,128)S(1)}, u32[]{:S(2)}, u32[]{:S(2)}) collective-permute-start(f32[5,5,160]{2,1,0:T(8,128)S(1)} %get-tuple-element.12), channel_id=1, source_target_pairs={{0,8},{8,16},{16,24},{24,0},{1,9},{9,17},{17,25},{25,1},{2,10},{10... | collective-permute-start | bytes 48008 | tf_op jit(solution)/shard_map/ppermute | solution.py:394
  33.2 6.9 %collective-permute-start.3 = (f32[5,5,160]{2,1,0:T(8,128)S(1)}, f32[5,5,160]{2,1,0:T(8,128)S(1)}, u32[]{:S(2)}, u32[]{:S(2)}) collective-permute-start(f32[5,5,160]{2,1,0:T(8,128)S(1)} %get-tuple-element.13), channel_id=1, source_target_pairs={{0,24},{8,0},{16,8},{24,16},{1,25},{9,1},{17,9},{25,17},{2,26},{10... | collective-permute-start | bytes 48008 | tf_op jit(solution)/shard_map/ppermute | solution.py:394
  34.2 10.3 %all-to-all-start.2 = ((f32[32,1,16]{2,1,0:T(1,128)}), f32[32,1,16]{2,1,0:T(1,128)S(1)}, u32[]{:S(2)}, u32[]{:S(2)}) async-start(f32[32,1,16]{2,1,0:T(1,128)} %shard_map.90), calls=%async_computation.2 | async-start | bytes 32768 | tf_op jit(solution)/shard_map/all_to_all | solution.py:404

commit v3 on v2

--- a/solution.py
+++ b/solution.py
@@ -15,7 +15,7 @@
 PAIR = ("gx", "gy")
 PLACE_FIRST = 21
 SHARE_FIRST = 4
-COLLECT_FIRST = 17
+COLLECT_FIRST = 21
 Z_ROWS = 10
 HINT_FLOPS = 20_000_000_000
 HINT_BYTES = 800_000_000
@@ -65,6 +65,10 @@
     return picked
 
 
+def is_even(axis, shape):
+    return (jnp.zeros(shape, jnp.int32) + lax.axis_index(axis)) & 1 == 0
+
+
 def flux4(rho, vel, pressure, d):
     mass = rho * vel[d]
     return [mass] + [mass * vel[m] + pressure if m == d else mass * vel[m] for m in range(3)]
@@ -80,7 +84,7 @@
                 grid[1 + m, x, y : y + 1, 0:nz] = vel[x, y, m : m + 1, :]
 
 
-def face_kernel(per_group, mask, den, vel, pre, sid, code, blocks, x_lo, x_hi, y_lo, y_hi, z_both, grid, rows):
+def face_kernel(per_group, mask, den, vel, pre, sid, code, blocks, x_one, x_two, y_one, y_two, z_both, grid, rows):
     nx, ny, nz = den.shape
     slots = sid.shape[1]
     groups = blocks.shape[0]
@@ -147,12 +151,15 @@
         placed += lax.dot_general(spread, lane_hot, (((1,), (1,)), ((), ())), preferred_element_type=F32)
     blocks[...] = placed.astype(BF16).reshape(groups, 16, 128)
 
+    even_x, even_y = is_even("gx", (ny, nz)), is_even("gy", (1, nz))
     for f in range(5):
-        x_lo[f] = grid[f, 0, 0:ny, 0:nz]
-        x_hi[f] = grid[f, nx - 1, 0:ny, 0:nz]
+        low, high = field(f, 0), field(f, nx - 1)
+        x_one[f] = jnp.where(even_x, high, low)
+        x_two[f] = jnp.where(even_x, low, high)
         for x in range(nx):
-            y_lo[f, x : x + 1] = grid[f, x, 0:1, 0:nz]
-            y_hi[f, x : x + 1] = grid[f, x, ny - 1 : ny, 0:nz]
+            low, high = grid[f, x, 0:1, 0:nz], grid[f, x, ny - 1 : ny, 0:nz]
+            y_one[f, x : x + 1] = jnp.where(even_y, high, low)
+            y_two[f, x : x + 1] = jnp.where(even_y, low, high)
 
     z_both[...] = F32(1) - mask[...]
     z_both[0:Z_ROWS] = jnp.zeros((Z_ROWS, 128), F32)
@@ -208,7 +215,7 @@
     return [rho, v1, v2, v3, pressure, specific, jnp.sqrt(F32(GAMMA) * ratio)]
 
 
-def tendency_kernel(start, blend, x_low, x_up, y_low, y_up, z_all, out, grid):
+def tendency_kernel(start, blend, x_one, x_two, y_one, y_two, z_all, out, grid):
     _, nx, ny, nz = out.shape
     shape = (8, LANES)
     grid[...] = jnp.ones_like(grid)
@@ -228,15 +235,17 @@
 
     z_low = from_layer(-1, 1)
     z_up = from_layer(1, 0)
+    even_x, even_y = is_even("gx", (ny, nz)), is_even("gy", (1, nz))
     half_lane = iota((8, 128), 1)
     outside = (iota((8, 128), 0) >= ny) & (half_lane >= nz - 128)
     for f in range(5):
-        grid[f, 0, 0:ny, 0:nz] = x_low[f]
-        grid[f, 1 + nx, 0:ny, 0:nz] = x_up[f]
+        grid[f, 0, 0:ny, 0:nz] = jnp.where(even_x, x_two[f], x_one[f])
+        grid[f, 1 + nx, 0:ny, 0:nz] = jnp.where(even_x, x_one[f], x_two[f])
         for x in range(nx):
             grid[f, 1 + x, 0:ny, 0:nz] = start[f, x, 0:ny, 0:nz]
-            grid[f, 1 + x, ny : ny + 1, 0:nz] = y_up[f, x : x + 1]
-            grid[f, 1 + x, 7:8, 0:nz] = y_low[f, x : x + 1]
+            one, two = y_one[f, x : x + 1], y_two[f, x : x + 1]
+            grid[f, 1 + x, ny : ny + 1, 0:nz] = jnp.where(even_y, one, two)
+            grid[f, 1 + x, 7:8, 0:nz] = jnp.where(even_y, two, one)
             at = 5 * f + x
             upper = grid[f, 1 + x, :, 128:256]
             upper = jnp.where(half_lane == nz - 128, pltpu.roll(z_up, (nz - 128 - at) % 128, 1), upper)
@@ -376,7 +385,7 @@
     codes = surface_face_code.reshape(1, -1)
     speeds = jnp.transpose(velocity, (1, 2, 0, 3))
     mask = call(mask_kernel, sds((16, 128), F32), [], flops=HINT_FLOPS, moved=HINT_BYTES)
-    blocks, x_lo, x_hi, y_lo, y_hi, z_both, grid = call(
+    blocks, x_one, x_two, y_one, y_two, z_both, grid = call(
         functools.partial(face_kernel, faces),
         [sds((groups, 16, 128), BF16)]
         + [sds((5, ny, nz), F32)] * 2
@@ -389,14 +398,15 @@
     )
     arrived = lax.all_to_all(blocks, PAIR, 0, 0, tiled=True, axis_index_groups=[rotated(groups, PLACE_FIRST)])
 
-    def shift(array, axis, step):
+    def swap(array, axis, first):
         peers = lax.axis_size(axis)
-        return lax.ppermute(array, axis, [(i, (i + step) % peers) for i in range(peers)])
-
-    x_low = shift(x_hi, "gx", 1)
-    x_up = shift(x_lo, "gx", -1)
-    y_low = shift(y_hi, "gy", 1)
-    y_up = shift(y_lo, "gy", -1)
+        step = lambda i: 1 if (i % 2 == 0) == first else -1
+        return lax.ppermute(array, axis, [(i, (i + step(i)) % peers) for i in range(peers)])
+
+    x_one = swap(x_one, "gx", True)
+    x_two = swap(x_two, "gx", False)
+    y_one = swap(y_one, "gy", True)
+    y_two = swap(y_two, "gy", False)
 
     copies = call(gather_kernel, sds((layers, 16, 128), BF16), [arrived, z_both], flops=HINT_FLOPS, moved=HINT_BYTES)
     everywhere = lax.all_to_all(copies, "gz", 0, 0, tiled=True, axis_index_groups=[rotated(layers, SHARE_FIRST)])
@@ -407,7 +417,7 @@
     tendency = call(
         tendency_kernel,
         sds((5, nx, ny, nz), F32),
-        [grid, blending.reshape(1, -1), x_low, x_up, y_low, y_up, everywhere],
+        [grid, blending.reshape(1, -1), x_one, x_two, y_one, y_two, everywhere],
         [pltpu.VMEM((5, nx + 2, 8, LANES), F32)],
         flops=20_000_000,
     )

time: 45.2 us -> 44.5 us (0.985)
  waiting for transfers between devices: 2.01 us -> 0.02 us
  starting transfers between devices: 23.6 us -> 24.8 us
    all_to_all x1, waiting for transfers between devices: 1.99 us -> 0.01 us  [step(): lax.all_to_all(partial, PAIR, 0, 0, tiled=True, axis_index_groups=[rotate...]
    all_to_all x1, starting transfers between devices: 5.86 us -> 7.2 us  [step(): lax.all_to_all(partial, PAIR, 0, 0, tiled=True, axis_index_groups=[rotate...]
  transfers between devices with their start and end apart: 6 -> 6, of which waited for: 1 -> 0; matrix products, arithmetic and copies ran while one was open for 0% -> 0% of each run, Pallas kernels for 7% -> 8%
where the time goes in v3:
time: 44.5 us; the launch traced here: 44.2 us
  starting transfers between devices  24.8 us (56%)
  blocking collectives  12.5 us (28%)
  Pallas kernels  5.25 us (12%)
  local copies, waits for them, and re-layouts  0.91 us (2%)
  between operations  0.74 us (2%)
    all_to_all x1, blocking collectives, step(): lax.all_to_all(blocks, PAIR, 0, 0, tiled=True, axis_index_groups=[rotated...  12.5 us
    all_to_all x1, starting transfers between devices, step(): lax.all_to_all(copies, 'gz', 0, 0, tiled=True, axis_index_groups=[rotated...  10.2 us
    ppermute x4, starting transfers between devices, swap(): lax.ppermute(array, axis, [(i, (i + step(i)) % peers) for i in range(peer...  7.35 us
    all_to_all x1, starting transfers between devices, step(): lax.all_to_all(partial, PAIR, 0, 0, tiled=True, axis_index_groups=[rotate...  7.2 us
    pallas_call x6, Pallas kernels, call(): pl.pallas_call(kernel, out_shape=outs, in_specs=[pl.BlockSpec(memory_spac...  5.25 us
    unnamed x14, local copies, waits for them, and re-layouts  0.91 us
  transfers between devices with their start and end apart: 6, of which 0 were waited for; matrix products, arithmetic and copies ran while one was open for 0% of the time, Pallas kernels for 8%

profile of v3, /device:TPU:1, one launch (start us, length us, event | category | flops | bytes accessed | tf_op | source)
XLA Modules:
  0.0 44.2 jit_solution(2531846001874332122)
XLA Ops:
  0.6 0.0 copy-start.5
  0.6 0.0 copy-start.4
  0.7 0.0 copy-start.3
  0.7 0.0 copy-start.1
  0.7 0.0 copy-start.2
  0.7 0.6 %copy-done.5 = s32[120]{0:T(128)S(1)} copy-done((s32[120]{0:T(128)S(1)}, s32[120]{0:T(128)}, u32[]{:S(2)}) %copy-start.5) | copy-done | bytes 504
  1.3 0.0 copy-done.4
  1.3 0.1 copy-done.3
  1.4 0.1 copy-done.1
  1.6 0.0 copy-done.2
  1.6 0.7 %shard_map.87 = (bf16[32,16,128]{2,1,0:T(8,128)(2,1)S(1)}, f32[5,5,160]{2,1,0:T(8,128)S(1)}, f32[5,5,160]{2,1,0:T(8,128)S(1)}, f32[5,5,160]{2,1,0:T(8,128)S(1)},...) custom-call(f32[16,128]{1,0:T(8,128)S(1)} %shard_map.86.mask, ...), custom_call_target="tpu_custom_call" | custom-call | flops 1000000 | bytes 200000 | tf_op jit(solution)/shard_map/pallas_call | solution.py:366
  2.3 12.5 %all_to_all.15.got = bf16[32,16,128]{2,1,0:T(8,128)(2,1)S(1)} all-to-all(bf16[32,16,128]{2,1,0:T(8,128)(2,1)S(1)} %get-tuple-element.14), channel_id=1, replica_groups={{168,176,184,192,200,208,216,224,232,240,248,0,8,16,24,32,40,48,56,64,7..., dimensions={0} | all-to-all | bytes 262144 | tf_op jit(solution)/shard_map/all_to_all | solution.py:399
  14.8 0.0 copy-start
  14.8 0.7 %shard_map.88 = bf16[8,16,128]{2,1,0:T(8,128)(2,1)} custom-call(bf16[32,16,128]{2,1,0:T(8,128)(2,1)S(1)} %all_to_all.15.got, f32[16,128]{1,0:T(8,128)S(1)} %get-tuple-element.15.z_both), custom_call_target="tpu_custom_call" | custom-call | flops 20000000000 | bytes 800000000 | tf_op jit(solution)/shard_map/pallas_call | solution.py:366
  15.4 0.0 copy-start.6
  15.4 10.2 %all-to-all-start.1 = ((bf16[8,16,128]{2,1,0:T(8,128)(2,1)}), bf16[8,16,128]{2,1,0:T(8,128)(2,1)S(1)}, u32[]{:S(2)}, u32[]{:S(2)}) async-start(bf16[8,16,128]{2,1,0:T(8,128)(2,1)} %shard_map.88), calls=%async_computation.1 | async-start | bytes 65536 | tf_op jit(solution)/shard_map/all_to_all | solution.py:412
  25.7 2.6 %collective-permute-start = (f32[5,5,160]{2,1,0:T(8,128)S(1)}, f32[5,5,160]{2,1,0:T(8,128)S(1)}, u32[]{:S(2)}, u32[]{:S(2)}) collective-permute-start(f32[5,5,160]{2,1,0:T(8,128)S(1)} %get-tuple-element.10), channel_id=1, source_target_pairs={{0,32},{32,0},{64,96},{96,64},{128,160},{160,128},{192,224},{224,1... | collective-permute-start | bytes 48008 | tf_op jit(solution)/shard_map/ppermute | solution.py:404
  28.3 2.3 %collective-permute-start.1 = (f32[5,5,160]{2,1,0:T(8,128)S(1)}, f32[5,5,160]{2,1,0:T(8,128)S(1)}, u32[]{:S(2)}, u32[]{:S(2)}) collective-permute-start(f32[5,5,160]{2,1,0:T(8,128)S(1)} %get-tuple-element.11), channel_id=1, source_target_pairs={{0,224},{32,64},{64,32},{96,128},{128,96},{160,192},{192,160},{224... | collective-permute-start | bytes 48008 | tf_op jit(solution)/shard_map/ppermute | solution.py:404
  30.6 1.4 %collective-permute-start.2 = (f32[5,5,160]{2,1,0:T(8,128)S(1)}, f32[5,5,160]{2,1,0:T(8,128)S(1)}, u32[]{:S(2)}, u32[]{:S(2)}) collective-permute-start(f32[5,5,160]{2,1,0:T(8,128)S(1)} %get-tuple-element.12), channel_id=1, source_target_pairs={{0,8},{8,0},{16,24},{24,16},{1,9},{9,1},{17,25},{25,17},{2,10},{10... | collective-permute-start | bytes 48008 | tf_op jit(solution)/shard_map/ppermute | solution.py:404
  32.0 1.1 %collective-permute-start.3 = (f32[5,5,160]{2,1,0:T(8,128)S(1)}, f32[5,5,160]{2,1,0:T(8,128)S(1)}, u32[]{:S(2)}, u32[]{:S(2)}) collective-permute-start(f32[5,5,160]{2,1,0:T(8,128)S(1)} %get-tuple-element.13), channel_id=1, source_target_pairs={{0,24},{8,16},{16,8},{24,0},{1,25},{9,17},{17,9},{25,1},{2,26},{10... | collective-permute-start | bytes 48008 | tf_op jit(solution)/shard_map/ppermute | solution.py:404
  33.0 0.0 all-to-all-done.1.z_all.got
  33.0 0.0 copy-done
  33.0 1.0 %shard_map.90 = f32[32,1,16]{2,1,0:T(1,128)} custom-call(bf16[8,16,128]{2,1,0:T(8,128)(2,1)S(1)} %all-to-all-done.1.z_all.got, bf16[4,320,512]{2,1,0:T(8,128)(2,1)S(1)} %copy-done), custom_call_target="tpu_custom_call" | custom-call | flops 1000000 | bytes 200000 | tf_op jit(solution)/shard_map/pallas_call | solution.py:366
  34.0 7.2 %all-to-all-start.2 = ((f32[32,1,16]{2,1,0:T(1,128)}), f32[32,1,16]{2,1,0:T(1,128)S(1)}, u32[]{:S(2)}, u32[]{:S(2)}) async-start(f32[32,1,16]{2,1,0:T(1,128)} %shard_map.90), calls=%async_computation.2 | async-start | bytes 32768 | tf_op jit(solution)/shard_map/all_to_all | solution.py:414
  41.2 0.0 collective-permute-done.x_one
  41.3 0.0 collective-permute-done.1.x_two
  41.3 0.0 collective-permute-done.2.y_one
  41.3 0.0 collective-permute-done.3.y_two
  41.3 0.0 copy-done.6
  41.3 2.3 %shard_map.89 = f32[5,5,5,160]{3,2,1,0:T(8,128)} custom-call(f32[5,5,8,256]{3,2,1,0:T(8,128)S(1)} %get-tuple-element.9.start, f32[1,32]{1,0:T(1,128)S(1)} %bitcast.8, f32[5,5,160]{2,1,0:T(8,128)S(1)} %collective-permute-done.x_one, f32[5,5,160]{2,1,0:T(8,128)S(1)} %collective-permute-done.1.x_two, f32[5,5,160]{2,1,0:T(8,128)S(1)} %collective-permute-done.2.y_one, ...), custom_call_target="tpu_custom_call" | custom-call | flops 20000000 | bytes 200000 | tf_op jit(solution)/shard_map/pallas_call | solution.py:366
  43.6 0.0 all-to-all-done.2.tiles
  43.6 0.5 %shard_map.91 = f32[1,16]{1,0:T(1,128)} custom-call(f32[32,1,16]{2,1,0:T(1,128)S(1)} %all-to-all-done.2.tiles), custom_call_target="tpu_custom_call" | custom-call | flops 1000000 | bytes 200000 | tf_op jit(solution)/shard_map/pallas_call | solution.py:366
  (1 shorter events, 0.0 us)
Async XLA Ops:
  0.6 0.7 %copy-start.5 = (s32[120]{0:T(128)S(1)}, s32[120]{0:T(128)}, u32[]{:S(2)}) copy-start(s32[120]{0:T(128)} %param.13) | copy-start | bytes 1444
  0.6 0.7 %copy-start.4 = (s32[120]{0:T(128)S(1)}, s32[120]{0:T(128)}, u32[]{:S(2)}) copy-start(s32[120]{0:T(128)} %param.12) | copy-start | bytes 1444
  0.7 0.8 %copy-start.3 = (f32[5,5,160]{2,1,0:T(8,128)S(1)}, f32[5,5,160]{2,1,0:T(8,128)}, u32[]{:S(2)}) copy-start(f32[5,5,160]{2,1,0:T(8,128)} %pre.1) | copy-start | bytes 48004
  0.7 0.9 %copy-start.1 = (f32[3,5,5,160]{3,0,2,1:T(4,128)S(1)}, f32[3,5,5,160]{3,0,2,1:T(4,128)}, u32[]{:S(2)}) copy-start(f32[3,5,5,160]{3,0,2,1:T(4,128)} %param.8) | copy-start | bytes 144004
  0.7 0.9 %copy-start.2 = (f32[5,5,160]{2,1,0:T(8,128)S(1)}, f32[5,5,160]{2,1,0:T(8,128)}, u32[]{:S(2)}) copy-start(f32[5,5,160]{2,1,0:T(8,128)} %den.1) | copy-start | bytes 48004
  14.8 18.2 %copy-start = (bf16[4,320,512]{2,1,0:T(8,128)(2,1)S(1)}, bf16[4,320,512]{2,1,0:T(8,128)(2,1)}, u32[]{:S(2)}) copy-start(bf16[4,320,512]{2,1,0:T(8,128)(2,1)} %weights.1) | copy-start | bytes 3932164
  15.4 25.8 %copy-start.6 = (f32[1,1,32]{2,1,0:T(1,128)S(1)}, f32[1,1,32]{2,1,0:T(1,128)}, u32[]{:S(2)}) copy-start(f32[1,1,32]{2,1,0:T(1,128)} %param.10) | copy-start | bytes 388
  15.4 17.6 %all-to-all-start.1 = ((bf16[8,16,128]{2,1,0:T(8,128)(2,1)}), bf16[8,16,128]{2,1,0:T(8,128)(2,1)S(1)}, u32[]{:S(2)}, u32[]{:S(2)}) async-start(bf16[8,16,128]{2,1,0:T(8,128)(2,1)} %shard_map.88), calls=%async_computation.1 | async-start | bytes 65536 | tf_op jit(solution)/shard_map/all_to_all | solution.py:412
  25.7 15.6 %collective-permute-start = (f32[5,5,160]{2,1,0:T(8,128)S(1)}, f32[5,5,160]{2,1,0:T(8,128)S(1)}, u32[]{:S(2)}, u32[]{:S(2)}) collective-permute-start(f32[5,5,160]{2,1,0:T(8,128)S(1)} %get-tuple-element.10), channel_id=1, source_target_pairs={{0,32},{32,0},{64,96},{96,64},{128,160},{160,128},{192,224},{224,1... | collective-permute-start | bytes 48008 | tf_op jit(solution)/shard_map/ppermute | solution.py:404
  28.3 12.9 %collective-permute-start.1 = (f32[5,5,160]{2,1,0:T(8,128)S(1)}, f32[5,5,160]{2,1,0:T(8,128)S(1)}, u32[]{:S(2)}, u32[]{:S(2)}) collective-permute-start(f32[5,5,160]{2,1,0:T(8,128)S(1)} %get-tuple-element.11), channel_id=1, source_target_pairs={{0,224},{32,64},{64,32},{96,128},{128,96},{160,192},{192,160},{224... | collective-permute-start | bytes 48008 | tf_op jit(solution)/shard_map/ppermute | solution.py:404
  30.6 10.7 %collective-permute-start.2 = (f32[5,5,160]{2,1,0:T(8,128)S(1)}, f32[5,5,160]{2,1,0:T(8,128)S(1)}, u32[]{:S(2)}, u32[]{:S(2)}) collective-permute-start(f32[5,5,160]{2,1,0:T(8,128)S(1)} %get-tuple-element.12), channel_id=1, source_target_pairs={{0,8},{8,0},{16,24},{24,16},{1,9},{9,1},{17,25},{25,17},{2,10},{10... | collective-permute-start | bytes 48008 | tf_op jit(solution)/shard_map/ppermute | solution.py:404
  32.0 9.3 %collective-permute-start.3 = (f32[5,5,160]{2,1,0:T(8,128)S(1)}, f32[5,5,160]{2,1,0:T(8,128)S(1)}, u32[]{:S(2)}, u32[]{:S(2)}) collective-permute-start(f32[5,5,160]{2,1,0:T(8,128)S(1)} %get-tuple-element.13), channel_id=1, source_target_pairs={{0,24},{8,16},{16,8},{24,0},{1,25},{9,17},{17,9},{25,1},{2,26},{10... | collective-permute-start | bytes 48008 | tf_op jit(solution)/shard_map/ppermute | solution.py:404
  34.0 9.6 %all-to-all-start.2 = ((f32[32,1,16]{2,1,0:T(1,128)}), f32[32,1,16]{2,1,0:T(1,128)S(1)}, u32[]{:S(2)}, u32[]{:S(2)}) async-start(f32[32,1,16]{2,1,0:T(1,128)} %shard_map.90), calls=%async_computation.2 | async-start | bytes 32768 | tf_op jit(solution)/shard_map/all_to_all | solution.py:414

commit v4 on v3

--- a/solution.py
+++ b/solution.py
@@ -86,7 +86,10 @@
 
 def face_kernel(per_group, mask, den, vel, pre, sid, code, blocks, x_one, x_two, y_one, y_two, z_both, grid, rows):
     nx, ny, nz = den.shape
-    slots = sid.shape[1]
+    empty = 128 - sid.shape[1]
+    slots = 128
+    codes = jnp.concatenate([code[...], jnp.zeros((1, empty), jnp.int32)], axis=1)
+    ids = jnp.concatenate([sid[...], jnp.full((1, empty), -1, jnp.int32)], axis=1)
     groups = blocks.shape[0]
     rows[...] = jnp.zeros_like(rows)
     lay_out(den, vel, pre, grid)
@@ -117,8 +120,8 @@
         rows[8 * q + 4 : 8 * q + 5, :] = -over_z
         rows[8 * q + 5 : 8 * q + 6, :] = over_z
 
-    face = lax.shift_right_logical(code[...], 5)
-    elem = code[...] & 31
+    face = lax.shift_right_logical(codes, 5)
+    elem = codes & 31
     z = iota((nz, slots), 0)
     z_elem = lax.shift_right_logical(z * 52429, 18)
     z_node = z - 5 * z_elem
@@ -131,13 +134,12 @@
         for q in range(4)
     ]
 
-    ids = sid[...]
     group = lax.shift_right_logical(jnp.maximum(ids, 0) * 6554, 21)
     offset = ids - per_group * group
     group = jnp.where(ids >= 0, (group + groups - PLACE_FIRST) & (groups - 1), -1)
     row = iota((16, slots), 0)
     group_of = iota((groups, 16, slots), 0)
-    placed = jnp.zeros((groups * 16, 128), F32)
+    sides, hots = [], []
     for shift in sorted({q * per_group % 128 for q in range(4)}):
         spread = jnp.zeros((16, slots), F32)
         for q in range(4):
@@ -146,9 +148,11 @@
                 spread = jnp.where(row == at, data[q], spread)
         spread = spread.astype(BF16).astype(F32)
         spread = jnp.where(group_of == group[None], spread[None], F32(0))
-        spread = spread.reshape(groups * 16, slots).astype(BF16)
-        lane_hot = (iota((128, slots), 0) == ((shift + offset) & 127)).astype(F32).astype(BF16)
-        placed += lax.dot_general(spread, lane_hot, (((1,), (1,)), ((), ())), preferred_element_type=F32)
+        sides.append(spread.reshape(groups * 16, slots).astype(BF16))
+        hots.append((iota((128, slots), 0) == ((shift + offset) & 127)).astype(F32).astype(BF16))
+    placed = lax.dot_general(
+        jnp.concatenate(sides, axis=1), jnp.concatenate(hots, axis=1), (((1,), (1,)), ((), ())), preferred_element_type=F32
+    )
     blocks[...] = placed.astype(BF16).reshape(groups, 16, 128)
 
     even_x, even_y = is_even("gx", (ny, nz)), is_even("gy", (1, nz))

time: 44.5 us -> 44.4 us (level)
  no operation moved by 1% of the time
where the time goes in v4:
time: 44.4 us; the launch traced here: 44.2 us
  starting transfers between devices  24.8 us (56%)
  blocking collectives  12.5 us (28%)
  Pallas kernels  5.23 us (12%)
  local copies, waits for them, and re-layouts  0.91 us (2%)
  between operations  0.74 us (2%)
    all_to_all x1, blocking collectives, step(): lax.all_to_all(blocks, PAIR, 0, 0, tiled=True, axis_index_groups=[rotated...  12.5 us
    all_to_all x1, starting transfers between devices, step(): lax.all_to_all(copies, 'gz', 0, 0, tiled=True, axis_index_groups=[rotated...  10.2 us
    ppermute x4, starting transfers between devices, swap(): lax.ppermute(array, axis, [(i, (i + step(i)) % peers) for i in range(peer...  7.35 us
    all_to_all x1, starting transfers between devices, step(): lax.all_to_all(partial, PAIR, 0, 0, tiled=True, axis_index_groups=[rotate...  7.2 us
    pallas_call x6, Pallas kernels, call(): pl.pallas_call(kernel, out_shape=outs, in_specs=[pl.BlockSpec(memory_spac...  5.23 us
    unnamed x14, local copies, waits for them, and re-layouts  0.91 us
  transfers between devices with their start and end apart: 6, of which 0 were waited for; matrix products, arithmetic and copies ran while one was open for 0% of the time, Pallas kernels for 8%

profile of v4, /device:TPU:1, one launch (start us, length us, event | category | flops | bytes accessed | tf_op | source)
XLA Modules:
  0.0 44.2 jit_solution(6711408675311302851)
XLA Ops:
  0.6 0.0 copy-start.5
  0.6 0.0 copy-start.4
  0.7 0.0 copy-start.3
  0.7 0.0 copy-start.1
  0.7 0.0 copy-start.2
  0.7 0.6 %copy-done.5 = s32[120]{0:T(128)S(1)} copy-done((s32[120]{0:T(128)S(1)}, s32[120]{0:T(128)}, u32[]{:S(2)}) %copy-start.5) | copy-done | bytes 504
  1.3 0.0 copy-done.4
  1.3 0.1 copy-done.3
  1.4 0.1 copy-done.1
  1.6 0.0 copy-done.2
  1.6 0.7 %shard_map.87 = (bf16[32,16,128]{2,1,0:T(8,128)(2,1)S(1)}, f32[5,5,160]{2,1,0:T(8,128)S(1)}, f32[5,5,160]{2,1,0:T(8,128)S(1)}, f32[5,5,160]{2,1,0:T(8,128)S(1)},...) custom-call(f32[16,128]{1,0:T(8,128)S(1)} %shard_map.86.mask, ...), custom_call_target="tpu_custom_call" | custom-call | flops 1000000 | bytes 200000 | tf_op jit(solution)/shard_map/pallas_call | solution.py:370
  2.3 12.5 %all_to_all.15.got = bf16[32,16,128]{2,1,0:T(8,128)(2,1)S(1)} all-to-all(bf16[32,16,128]{2,1,0:T(8,128)(2,1)S(1)} %get-tuple-element.14), channel_id=1, replica_groups={{168,176,184,192,200,208,216,224,232,240,248,0,8,16,24,32,40,48,56,64,7..., dimensions={0} | all-to-all | bytes 262144 | tf_op jit(solution)/shard_map/all_to_all | solution.py:403
  14.8 0.0 copy-start
  14.8 0.7 %shard_map.88 = bf16[8,16,128]{2,1,0:T(8,128)(2,1)} custom-call(bf16[32,16,128]{2,1,0:T(8,128)(2,1)S(1)} %all_to_all.15.got, f32[16,128]{1,0:T(8,128)S(1)} %get-tuple-element.15.z_both), custom_call_target="tpu_custom_call" | custom-call | flops 20000000000 | bytes 800000000 | tf_op jit(solution)/shard_map/pallas_call | solution.py:370
  15.4 0.0 copy-start.6
  15.4 10.2 %all-to-all-start.1 = ((bf16[8,16,128]{2,1,0:T(8,128)(2,1)}), bf16[8,16,128]{2,1,0:T(8,128)(2,1)S(1)}, u32[]{:S(2)}, u32[]{:S(2)}) async-start(bf16[8,16,128]{2,1,0:T(8,128)(2,1)} %shard_map.88), calls=%async_computation.1 | async-start | bytes 65536 | tf_op jit(solution)/shard_map/all_to_all | solution.py:416
  25.7 2.6 %collective-permute-start = (f32[5,5,160]{2,1,0:T(8,128)S(1)}, f32[5,5,160]{2,1,0:T(8,128)S(1)}, u32[]{:S(2)}, u32[]{:S(2)}) collective-permute-start(f32[5,5,160]{2,1,0:T(8,128)S(1)} %get-tuple-element.10), channel_id=1, source_target_pairs={{0,32},{32,0},{64,96},{96,64},{128,160},{160,128},{192,224},{224,1... | collective-permute-start | bytes 48008 | tf_op jit(solution)/shard_map/ppermute | solution.py:408
  28.3 2.3 %collective-permute-start.1 = (f32[5,5,160]{2,1,0:T(8,128)S(1)}, f32[5,5,160]{2,1,0:T(8,128)S(1)}, u32[]{:S(2)}, u32[]{:S(2)}) collective-permute-start(f32[5,5,160]{2,1,0:T(8,128)S(1)} %get-tuple-element.11), channel_id=1, source_target_pairs={{0,224},{32,64},{64,32},{96,128},{128,96},{160,192},{192,160},{224... | collective-permute-start | bytes 48008 | tf_op jit(solution)/shard_map/ppermute | solution.py:408
  30.6 1.4 %collective-permute-start.2 = (f32[5,5,160]{2,1,0:T(8,128)S(1)}, f32[5,5,160]{2,1,0:T(8,128)S(1)}, u32[]{:S(2)}, u32[]{:S(2)}) collective-permute-start(f32[5,5,160]{2,1,0:T(8,128)S(1)} %get-tuple-element.12), channel_id=1, source_target_pairs={{0,8},{8,0},{16,24},{24,16},{1,9},{9,1},{17,25},{25,17},{2,10},{10... | collective-permute-start | bytes 48008 | tf_op jit(solution)/shard_map/ppermute | solution.py:408
  31.9 1.1 %collective-permute-start.3 = (f32[5,5,160]{2,1,0:T(8,128)S(1)}, f32[5,5,160]{2,1,0:T(8,128)S(1)}, u32[]{:S(2)}, u32[]{:S(2)}) collective-permute-start(f32[5,5,160]{2,1,0:T(8,128)S(1)} %get-tuple-element.13), channel_id=1, source_target_pairs={{0,24},{8,16},{16,8},{24,0},{1,25},{9,17},{17,9},{25,1},{2,26},{10... | collective-permute-start | bytes 48008 | tf_op jit(solution)/shard_map/ppermute | solution.py:408
  33.0 0.0 all-to-all-done.1.z_all.got
  33.0 0.0 copy-done
  33.0 1.0 %shard_map.90 = f32[32,1,16]{2,1,0:T(1,128)} custom-call(bf16[8,16,128]{2,1,0:T(8,128)(2,1)S(1)} %all-to-all-done.1.z_all.got, bf16[4,320,512]{2,1,0:T(8,128)(2,1)S(1)} %copy-done), custom_call_target="tpu_custom_call" | custom-call | flops 1000000 | bytes 200000 | tf_op jit(solution)/shard_map/pallas_call | solution.py:370
  34.0 7.2 %all-to-all-start.2 = ((f32[32,1,16]{2,1,0:T(1,128)}), f32[32,1,16]{2,1,0:T(1,128)S(1)}, u32[]{:S(2)}, u32[]{:S(2)}) async-start(f32[32,1,16]{2,1,0:T(1,128)} %shard_map.90), calls=%async_computation.2 | async-start | bytes 32768 | tf_op jit(solution)/shard_map/all_to_all | solution.py:418
  41.2 0.0 collective-permute-done.x_one
  41.2 0.0 collective-permute-done.1.x_two
  41.3 0.0 collective-permute-done.2.y_one
  41.3 0.0 collective-permute-done.3.y_two
  41.3 0.0 copy-done.6
  41.3 2.3 %shard_map.89 = f32[5,5,5,160]{3,2,1,0:T(8,128)} custom-call(f32[5,5,8,256]{3,2,1,0:T(8,128)S(1)} %get-tuple-element.9.start, f32[1,32]{1,0:T(1,128)S(1)} %bitcast.8, f32[5,5,160]{2,1,0:T(8,128)S(1)} %collective-permute-done.x_one, f32[5,5,160]{2,1,0:T(8,128)S(1)} %collective-permute-done.1.x_two, f32[5,5,160]{2,1,0:T(8,128)S(1)} %collective-permute-done.2.y_one, ...), custom_call_target="tpu_custom_call" | custom-call | flops 20000000 | bytes 200000 | tf_op jit(solution)/shard_map/pallas_call | solution.py:370
  43.6 0.0 all-to-all-done.2.tiles
  43.6 0.5 %shard_map.91 = f32[1,16]{1,0:T(1,128)} custom-call(f32[32,1,16]{2,1,0:T(1,128)S(1)} %all-to-all-done.2.tiles), custom_call_target="tpu_custom_call" | custom-call | flops 1000000 | bytes 200000 | tf_op jit(solution)/shard_map/pallas_call | solution.py:370
  (1 shorter events, 0.0 us)
Async XLA Ops:
  0.6 0.7 %copy-start.5 = (s32[120]{0:T(128)S(1)}, s32[120]{0:T(128)}, u32[]{:S(2)}) copy-start(s32[120]{0:T(128)} %param.13) | copy-start | bytes 1444
  0.6 0.7 %copy-start.4 = (s32[120]{0:T(128)S(1)}, s32[120]{0:T(128)}, u32[]{:S(2)}) copy-start(s32[120]{0:T(128)} %param.12) | copy-start | bytes 1444
  0.7 0.8 %copy-start.3 = (f32[5,5,160]{2,1,0:T(8,128)S(1)}, f32[5,5,160]{2,1,0:T(8,128)}, u32[]{:S(2)}) copy-start(f32[5,5,160]{2,1,0:T(8,128)} %pre.1) | copy-start | bytes 48004
  0.7 0.9 %copy-start.1 = (f32[3,5,5,160]{3,0,2,1:T(4,128)S(1)}, f32[3,5,5,160]{3,0,2,1:T(4,128)}, u32[]{:S(2)}) copy-start(f32[3,5,5,160]{3,0,2,1:T(4,128)} %param.8) | copy-start | bytes 144004
  0.7 0.9 %copy-start.2 = (f32[5,5,160]{2,1,0:T(8,128)S(1)}, f32[5,5,160]{2,1,0:T(8,128)}, u32[]{:S(2)}) copy-start(f32[5,5,160]{2,1,0:T(8,128)} %den.1) | copy-start | bytes 48004
  14.8 18.2 %copy-start = (bf16[4,320,512]{2,1,0:T(8,128)(2,1)S(1)}, bf16[4,320,512]{2,1,0:T(8,128)(2,1)}, u32[]{:S(2)}) copy-start(bf16[4,320,512]{2,1,0:T(8,128)(2,1)} %weights.1) | copy-start | bytes 3932164
  15.4 25.8 %copy-start.6 = (f32[1,1,32]{2,1,0:T(1,128)S(1)}, f32[1,1,32]{2,1,0:T(1,128)}, u32[]{:S(2)}) copy-start(f32[1,1,32]{2,1,0:T(1,128)} %param.10) | copy-start | bytes 388
  15.4 17.6 %all-to-all-start.1 = ((bf16[8,16,128]{2,1,0:T(8,128)(2,1)}), bf16[8,16,128]{2,1,0:T(8,128)(2,1)S(1)}, u32[]{:S(2)}, u32[]{:S(2)}) async-start(bf16[8,16,128]{2,1,0:T(8,128)(2,1)} %shard_map.88), calls=%async_computation.1 | async-start | bytes 65536 | tf_op jit(solution)/shard_map/all_to_all | solution.py:416
  25.7 15.6 %collective-permute-start = (f32[5,5,160]{2,1,0:T(8,128)S(1)}, f32[5,5,160]{2,1,0:T(8,128)S(1)}, u32[]{:S(2)}, u32[]{:S(2)}) collective-permute-start(f32[5,5,160]{2,1,0:T(8,128)S(1)} %get-tuple-element.10), channel_id=1, source_target_pairs={{0,32},{32,0},{64,96},{96,64},{128,160},{160,128},{192,224},{224,1... | collective-permute-start | bytes 48008 | tf_op jit(solution)/shard_map/ppermute | solution.py:408
  28.3 12.9 %collective-permute-start.1 = (f32[5,5,160]{2,1,0:T(8,128)S(1)}, f32[5,5,160]{2,1,0:T(8,128)S(1)}, u32[]{:S(2)}, u32[]{:S(2)}) collective-permute-start(f32[5,5,160]{2,1,0:T(8,128)S(1)} %get-tuple-element.11), channel_id=1, source_target_pairs={{0,224},{32,64},{64,32},{96,128},{128,96},{160,192},{192,160},{224... | collective-permute-start | bytes 48008 | tf_op jit(solution)/shard_map/ppermute | solution.py:408
  30.6 10.7 %collective-permute-start.2 = (f32[5,5,160]{2,1,0:T(8,128)S(1)}, f32[5,5,160]{2,1,0:T(8,128)S(1)}, u32[]{:S(2)}, u32[]{:S(2)}) collective-permute-start(f32[5,5,160]{2,1,0:T(8,128)S(1)} %get-tuple-element.12), channel_id=1, source_target_pairs={{0,8},{8,0},{16,24},{24,16},{1,9},{9,1},{17,25},{25,17},{2,10},{10... | collective-permute-start | bytes 48008 | tf_op jit(solution)/shard_map/ppermute | solution.py:408
  31.9 9.3 %collective-permute-start.3 = (f32[5,5,160]{2,1,0:T(8,128)S(1)}, f32[5,5,160]{2,1,0:T(8,128)S(1)}, u32[]{:S(2)}, u32[]{:S(2)}) collective-permute-start(f32[5,5,160]{2,1,0:T(8,128)S(1)} %get-tuple-element.13), channel_id=1, source_target_pairs={{0,24},{8,16},{16,8},{24,0},{1,25},{9,17},{17,9},{25,1},{2,26},{10... | collective-permute-start | bytes 48008 | tf_op jit(solution)/shard_map/ppermute | solution.py:408
  34.0 9.6 %all-to-all-start.2 = ((f32[32,1,16]{2,1,0:T(1,128)}), f32[32,1,16]{2,1,0:T(1,128)S(1)}, u32[]{:S(2)}, u32[]{:S(2)}) async-start(f32[32,1,16]{2,1,0:T(1,128)} %shard_map.90), calls=%async_computation.2 | async-start | bytes 32768 | tf_op jit(solution)/shard_map/all_to_all | solution.py:418
